TPU v7x, 32 devices: a whole 2x2x4 slice. The times are simulated.
32 devices in a mesh: fsdp: 8 (over y, x, core), seq: 4 (over z).
Axes of the slice: x: 2, y: 2, z: 4, core: 2. Of those that a mesh axis runs over, the one named last changes fastest.
Arguments:
- tokens: bfloat16 [8, 2048, 4096], P('fsdp', 'seq'), may hold values from -72 to 72
- norm_gain: float32 [4096], replicated, may hold values from 0.1 to 1.9
- lru_proj: bfloat16 [4096, 2048], P(('fsdp', 'seq')), may hold values from -0.09375 to 0.09375
- gelu_proj: bfloat16 [4096, 2048], P(('fsdp', 'seq')), may hold values from -0.09375 to 0.09375
- conv_weight: float32 [4, 2048], replicated, may hold values from -3 to 3
- conv_bias: float32 [2048], replicated, may hold values from -3 to 3
- gate_weights: bfloat16 [2048, 512], P('seq'), may hold values from -0.375 to 0.375
- gate_bias: float32 [2, 2048], replicated, may hold values from -4 to 4
- decay_param: float32 [2048], replicated, may hold values from -13 to -2
Outputs:
- recurrent_out: bfloat16 [8, 2048, 2048], P('fsdp', 'seq')
All inputs are finite; a program needn't handle non-finite values.
Results may differ from a plain program's by a relative error of at most 0.0051.
Values may be sent and summed in bfloat16 or wider, within the bound.
A program may use at most 128 MiB of HBM per device.

v0:
```python
import functools

import jax
import jax.numpy as jnp
from jax import lax
from jax.experimental import pallas as pl
from jax.experimental.pallas import tpu as pltpu
from jax.sharding import PartitionSpec as P

MESH = pl.DeviceIdType.MESH
LANES = 128
VMEM_BYTES = 66_000_000


def normalise(tokens_ref, gain_ref, normed_ref, part, parts):
    rows = 32

    def body(i, _):
        at = pl.ds(pl.multiple_of(i * rows, rows), rows)
        values = tokens_ref[at, :].astype(jnp.float32)
        mean_square = jnp.mean(values * values, axis=-1, keepdims=True)
        normed_ref[at, :] = (values * lax.rsqrt(mean_square + 1e-06) * gain_ref[...]).astype(jnp.bfloat16)
        return 0

    blocks = tokens_ref.shape[0] // rows // parts
    lax.fori_loop(part * blocks, (part + 1) * blocks, body, 0)


def branch_kernel(
    nz,
    tokens_ref, gain_ref, lru_ref, gelu_ref, gate_ref,
    weight_ref, bias_ref, gate_bias_ref, decay_ref,
    out_ref,
    w_ref, normed_ref, rec_ref, table_ref, before_ref, padded_ref, a_ref, b_ref,
    end_ref, carry_ref, start_ref,
    own_sem, send_sem, core_send, gate_send, gate_core_send, tail_send, carry_send,
    z_recv, gate_recv, gate_core_recv, x_recv, y_recv, a_recv, b_recv, core_recv,
    tail_recv, carry_recv,
):
    f = lax.axis_index("fsdp")
    z = lax.axis_index("seq")
    c, x, y = f % 2, (f // 2) % 2, f // 4
    fx, fy, fc = f + 2 - 4 * x, f + 4 - 8 * y, f + 1 - 2 * c
    fd = fx + 4 - 8 * y
    shard = lru_ref.shape[0]
    line = shard * nz
    half = line // 2
    chunks = w_ref.shape[0]
    split = chunks // 2
    gate_rows = gate_ref.shape[0]
    gate_steps = split // 2
    piece = gate_rows // 2 // gate_steps
    rows = normed_ref.shape[0]
    channels = table_ref.shape[1] // 2
    heads = rec_ref.shape[1] // channels
    pieces = channels // LANES
    taps = weight_ref.shape[0]
    lead = before_ref.shape[0]

    def remote(src, send, recv, device):
        return pltpu.make_async_remote_copy(
            src_ref=src, dst_ref=src, send_sem=send, recv_sem=recv,
            device_id=device, device_id_type=MESH,
        )

    own = pl.ds(pl.multiple_of((f * nz + z) * shard, shard), shard)
    for t in range(chunks):
        src = lru_ref if t < split else gelu_ref
        cols = pl.ds((t % split) * LANES, LANES)
        pltpu.make_async_copy(src.at[:, cols], w_ref.at[t, own], own_sem.at[0]).start()
    own_gate = pl.ds(pl.multiple_of(z * gate_rows, gate_rows), gate_rows)
    gate_copy = pltpu.make_async_copy(gate_ref, table_ref.at[own_gate], own_sem.at[1])
    gate_copy.start()

    barrier = pltpu.get_barrier_semaphore()
    for device in ((fx, z), (fy, z), (fc, z)):
        pl.semaphore_signal(barrier, inc=1, device_id=device, device_id_type=MESH)

    @pl.when(z > 0)
    def _():
        pl.semaphore_signal(barrier, inc=1, device_id=(f, z - 1), device_id_type=MESH)

    @pl.when(z < nz - 1)
    def _():
        pl.semaphore_signal(barrier, inc=1, device_id=(f, z + 1), device_id_type=MESH)

    for k in range(nz):
        @pl.when(z == k)
        def _():
            pl.semaphore_wait(barrier, 3 + int(k > 0) + int(k < nz - 1))

    pltpu.make_async_copy(w_ref.at[:, own], w_ref.at[:, own], own_sem.at[0]).wait()
    gate_copy.wait()

    def shard_of(t, source):
        at = pl.ds(pl.multiple_of((f * nz + source) * shard, shard), shard)
        return w_ref.at[t, at]

    def gate_of(t, source):
        first = source * gate_rows + c * (gate_rows // 2) + t * piece
        return table_ref.at[pl.ds(pl.multiple_of(first, piece), piece)]

    def pass_on(t, source, target):
        remote(shard_of(t, source), send_sem.at[t], z_recv.at[t, source], (f, target)).start()

        @pl.when(t < gate_steps)
        def _():
            remote(gate_of(t, source), gate_send.at[t], gate_recv.at[t, source], (f, target)).start()

    def arrived(t, source):
        remote(shard_of(t, source), send_sem.at[t], z_recv.at[t, source], (f, z)).wait_recv()

        @pl.when(t < gate_steps)
        def _():
            remote(gate_of(t, source), gate_send.at[t], gate_recv.at[t, source], (f, z)).wait_recv()

    def z_first(t):
        @pl.when(z > 0)
        def _():
            pass_on(t, z, z - 1)

        @pl.when(z < nz - 1)
        def _():
            pass_on(t, z, z + 1)

    def z_hop(t, distance):
        @pl.when(z >= distance)
        def _():
            arrived(t, z - distance)

            @pl.when(z < nz - 1)
            def _():
                pass_on(t, z - distance, z + 1)

        @pl.when(z + distance < nz)
        def _():
            arrived(t, z + distance)

            @pl.when(z > 0)
            def _():
                pass_on(t, z + distance, z - 1)

    def rows_of(owner, t, start, size):
        return w_ref.at[t, pl.ds(pl.multiple_of(owner * line + start, shard), size)]

    def to_core(t, owner, start, size):
        remote(rows_of(owner, t, start, size), core_send.at[t], core_recv.at[t], (fc, z)).start()

    def line_done(t):
        mine = rows_of(f, t, 0, line)
        remote(mine, send_sem.at[t], x_recv.at[t], (fx, z)).start()
        remote(mine, send_sem.at[t], y_recv.at[t], (fy, z)).start()
        to_core(t, f, 0, line)

        @pl.when(t < gate_steps)
        def _():
            for source in range(nz):
                @pl.when(z != source)
                def _():
                    remote(
                        gate_of(t, source), gate_core_send.at[t], gate_core_recv.at[t], (fc, z)
                    ).start()

    def gate_done(t):
        @pl.when(t < gate_steps)
        def _():
            others = table_ref.at[pl.ds(0, (nz - 1) * piece)]
            pltpu.make_async_copy(others, others, gate_core_recv.at[t]).wait()

    def sides_done(t):
        from_x = rows_of(fx, t, 0, line)
        remote(from_x, send_sem.at[t], x_recv.at[t], (fx, z)).wait_recv()
        remote(rows_of(fx, t, 0, half), send_sem.at[t], a_recv.at[t], (fy, z)).start()
        to_core(t, fx, 0, line)
        from_y = rows_of(fy, t, 0, line)
        remote(from_y, send_sem.at[t], y_recv.at[t], (fy, z)).wait_recv()
        remote(rows_of(fy, t, half, half), send_sem.at[t], b_recv.at[t], (fx, z)).start()
        to_core(t, fy, 0, line)

    def corner_done(t):
        remote(rows_of(fd, t, 0, half), send_sem.at[t], a_recv.at[t], (fy, z)).wait_recv()
        to_core(t, fd, 0, half)
        remote(rows_of(fd, t, half, half), send_sem.at[t], b_recv.at[t], (fx, z)).wait_recv()
        to_core(t, fd, half, half)

    def multiply(t):
        whole = w_ref.at[t, pl.ds(0, 4 * line)]
        pltpu.make_async_copy(whole, whole, core_recv.at[t]).wait()
        blocks = normed_ref.shape[0] // 512
        column = pl.ds(pl.multiple_of((t % split) * LANES, LANES), LANES)

        def body(i, _):
            at = pl.ds(pl.multiple_of(i * 512, 512), 512)
            product = jnp.dot(normed_ref[at, :], w_ref[t], preferred_element_type=jnp.float32)

            @pl.when(t < split)
            def _():
                rec_ref[at, column] = product.astype(jnp.bfloat16)

            @pl.when(t >= split)
            def _():
                chunk = jnp.maximum(t - split, 0)
                state = b_ref[chunk, at, :] + a_ref[chunk, at, :] * start_ref[0:1, column]
                out_ref[at, column] = (state * jax.nn.gelu(product, approximate=True)).astype(out_ref.dtype)

            return 0

        lax.fori_loop(0, blocks, body, 0)

    def columns(h):
        return pl.ds(pl.multiple_of(h * channels, channels), channels)

    def tail_copy(h, source_rows, device):
        return pltpu.make_async_remote_copy(
            src_ref=rec_ref.at[pl.ds(source_rows, lead), columns(h)],
            dst_ref=before_ref.at[:, columns(h)],
            send_sem=tail_send.at[h], recv_sem=tail_recv.at[h],
            device_id=device, device_id_type=MESH,
        )

    def carry_copy(h, device):
        return pltpu.make_async_remote_copy(
            src_ref=carry_ref.at[:, columns(h)], dst_ref=start_ref.at[:, columns(h)],
            send_sem=carry_send.at[h], recv_sem=carry_recv.at[h],
            device_id=device, device_id_type=MESH,
        )

    def send_tail(h):
        @pl.when(z < nz - 1)
        def _():
            tail_copy(h, rows - lead, (f, z + 1)).start()

    def scan(h):
        @pl.when(z > 0)
        def _():
            tail_copy(h, rows - lead, (f, z)).wait_recv()

        cols = columns(h)
        padded_ref[pl.ds(0, lead), :] = before_ref[:, cols].astype(jnp.float32)
        padded_ref[pl.ds(lead, rows), :] = rec_ref[:, cols].astype(jnp.float32)
        conv_sum = jnp.zeros((rows, channels), jnp.float32) + bias_ref[:, cols]
        for tap in range(taps):
            conv_sum = conv_sum + weight_ref[tap : tap + 1, cols] * padded_ref[pl.ds(lead - tap, rows), :]
        conv_out = conv_sum.astype(jnp.bfloat16)
        gates = jnp.dot(conv_out, table_ref[cols, :], preferred_element_type=jnp.float32)
        input_gate = jax.nn.sigmoid(gates[:, :channels] + gate_bias_ref[0:1, cols])
        recur_gate = jax.nn.sigmoid(gates[:, channels:] + gate_bias_ref[1:2, cols])
        param = decay_ref[:, cols]
        softplus = jnp.maximum(param, 0.0) + jnp.log1p(jnp.exp(-jnp.abs(param)))
        log_decay = -8.0 * softplus * recur_gate
        decay = jnp.exp(log_decay)
        lost = -jnp.tanh(log_decay) * (decay * decay + 1.0)
        driven = jnp.sqrt(lost) * input_gate * conv_out.astype(jnp.float32)
        for j in range(pieces):
            a_ref[h * pieces + j] = decay[:, j * LANES : (j + 1) * LANES]
            b_ref[h * pieces + j] = driven[:, j * LANES : (j + 1) * LANES]

        lanes = 8
        length = rows // lanes

        def body(i, carry):
            at = pl.ds(i, lanes, stride=length)
            after = []
            for j in range(pieces):
                product, state = carry[j]
                decay_now = a_ref[h * pieces + j, at, :]
                product = product * decay_now
                state = decay_now * state + b_ref[h * pieces + j, at, :]
                a_ref[h * pieces + j, at, :] = product
                b_ref[h * pieces + j, at, :] = state
                after.append((product, state))
            return tuple(after)

        fresh = (jnp.ones((lanes, LANES), jnp.float32), jnp.zeros((lanes, LANES), jnp.float32))
        totals = lax.fori_loop(0, length, body, (fresh,) * pieces, unroll=8)
        for j in range(pieces):
            product, state = totals[j]
            start = jnp.zeros((1, LANES), jnp.float32)
            prefix = jnp.ones((1, LANES), jnp.float32)
            for i in range(lanes):
                at = pl.ds(i * length, length)
                within = a_ref[h * pieces + j, at, :]
                b_ref[h * pieces + j, at, :] = b_ref[h * pieces + j, at, :] + within * start
                a_ref[h * pieces + j, at, :] = within * prefix
                start = product[i : i + 1, :] * start + state[i : i + 1, :]
                prefix = prefix * product[i : i + 1, :]
            col = pl.ds(pl.multiple_of((h * pieces + j) * LANES, LANES), LANES)
            end_ref[0:1, col] = prefix
            end_ref[1:2, col] = start

    def make_carry(h):
        cols = columns(h)

        @pl.when(z > 0)
        def _():
            carry_copy(h, (f, z)).wait_recv()

        @pl.when(z < nz - 1)
        def _():
            end = end_ref[0:1, cols] * start_ref[0:1, cols] + end_ref[1:2, cols]
            carry_ref[:, cols] = jnp.broadcast_to(end, (carry_ref.shape[0], channels))

    def send_carry(h):
        @pl.when(z < nz - 1)
        def _():
            carry_copy(h, (f, z + 1)).start()

    @pl.when(z == 0)
    def _():
        before_ref[...] = jnp.zeros_like(before_ref)
        start_ref[...] = jnp.zeros_like(start_ref)

    stages = [z_first]
    for distance in range(1, nz):
        stages.append(functools.partial(z_hop, distance=distance))
    stages += [line_done, sides_done, corner_done, gate_done, multiply]
    lags = list(range(nz)) + [nz - 1, nz, nz + 1, nz + 1, nz + 2]
    scan_at = gate_steps + nz

    def on_head(s, first, stage):
        @pl.when((s >= first) & (s < first + pieces * heads) & ((s - first) % pieces == 0))
        def _():
            stage((s - first) // pieces)

    def step(s, _):
        for stage, lag in zip(stages[:-1], lags[:-1]):
            @pl.when((s >= lag) & (s < chunks + lag))
            def _():
                stage(s - lag)

        on_head(s, scan_at + 2 + 2 * z, send_carry)
        on_head(s, nz + 2 + pieces, send_tail)

        @pl.when(s < 4)
        def _():
            normalise(tokens_ref, gain_ref, normed_ref, s, 4)

        on_head(s, scan_at + 1 + 2 * z, make_carry)

        @pl.when((s >= lags[-1]) & (s < chunks + lags[-1]))
        def _():
            multiply(s - lags[-1])

        on_head(s, scan_at, scan)
        return 0

    lax.fori_loop(0, chunks + lags[-1], step, 0)

    def drain(t, _):
        for k in range(nz):
            shards_sent = (k + 1 if k < nz - 1 else 0) + (nz - k if k > 0 else 0)

            @pl.when(z == k)
            def _():
                sent = w_ref.at[t, pl.ds(0, shards_sent * shard + 3 * line)]
                pltpu.make_async_copy(sent, sent, send_sem.at[t]).wait()

                @pl.when(t < gate_steps)
                def _():
                    sent_gate = table_ref.at[pl.ds(0, shards_sent * piece)]
                    pltpu.make_async_copy(sent_gate, sent_gate, gate_send.at[t]).wait()

        whole = w_ref.at[t, pl.ds(0, 4 * line)]
        pltpu.make_async_copy(whole, whole, core_send.at[t]).wait()

        @pl.when(t < gate_steps)
        def _():
            others = table_ref.at[pl.ds(0, (nz - 1) * piece)]
            pltpu.make_async_copy(others, others, gate_core_send.at[t]).wait()

        @pl.when((t < heads) & (z < nz - 1))
        def _():
            tail_copy(t, rows - lead, (f, z)).wait_send()
            carry_copy(t, (f, z)).wait_send()

        return 0

    lax.fori_loop(0, chunks, drain, 0)


def fused_branch(
    nz, tokens, norm_gain, lru_proj, gelu_proj, conv_weight, conv_bias, gate_weights, gate_bias,
    decay_param,
):
    rows, width = tokens.shape
    inner = lru_proj.shape[1]
    chunks = 2 * inner // LANES
    channels = gate_weights.shape[1] // 2
    heads = inner // channels
    vmem = pl.BlockSpec(memory_space=pltpu.VMEM)
    any_ = pl.BlockSpec(memory_space=pl.ANY)
    dma = pltpu.SemaphoreType.DMA
    f32, bf16 = jnp.float32, jnp.bfloat16
    lead = 16
    return pl.pallas_call(
        functools.partial(branch_kernel, nz),
        out_shape=jax.ShapeDtypeStruct((rows, inner), bf16),
        in_specs=[vmem, vmem, any_, any_, any_, vmem, vmem, vmem, vmem],
        out_specs=vmem,
        scratch_shapes=[
            pltpu.VMEM((chunks, width, LANES), bf16),
            pltpu.VMEM((rows, width), bf16),
            pltpu.VMEM((rows, inner), bf16),
            pltpu.VMEM((gate_weights.shape[0] * nz, 2 * channels), bf16),
            pltpu.VMEM((lead, inner), bf16),
            pltpu.VMEM((lead + rows, channels), f32),
            pltpu.VMEM((chunks // 2, rows, LANES), f32),
            pltpu.VMEM((chunks // 2, rows, LANES), f32),
            pltpu.VMEM((8, inner), f32), pltpu.VMEM((8, inner), f32), pltpu.VMEM((8, inner), f32),
            dma((2,)), dma((chunks,)), dma((chunks,)), dma((chunks // 4,)), dma((chunks // 4,)),
            dma((heads,)), dma((heads,)),
            dma((chunks, nz)), dma((chunks // 4, nz)), dma((chunks // 4,)),
            dma((chunks,)), dma((chunks,)), dma((chunks,)), dma((chunks,)), dma((chunks,)),
            dma((heads,)), dma((heads,)),
        ],
        compiler_params=pltpu.CompilerParams(
            collective_id=0, has_side_effects=True, vmem_limit_bytes=VMEM_BYTES
        ),
    )(
        tokens, norm_gain.reshape(1, width), lru_proj, gelu_proj, gate_weights, conv_weight,
        conv_bias.reshape(1, inner), gate_bias, decay_param.reshape(1, inner),
    )


def scan_kernel(
    rec_ref, before_ref, weight_ref, bias_ref, table_ref, gate_bias_ref, decay_ref,
    state_ref, cumulative_ref, end_ref, padded_ref, a_ref, b_ref,
):
    rows, channels = rec_ref.shape
    taps = weight_ref.shape[0]
    lead = before_ref.shape[0]
    padded_ref[pl.ds(0, lead), :] = before_ref[...].astype(jnp.float32)
    padded_ref[pl.ds(lead, rows), :] = rec_ref[...].astype(jnp.float32)
    conv_sum = jnp.zeros((rows, channels), jnp.float32) + bias_ref[...]
    for tap in range(taps):
        conv_sum = conv_sum + weight_ref[tap : tap + 1, :] * padded_ref[pl.ds(lead - tap, rows), :]
    conv_out = conv_sum.astype(jnp.bfloat16)
    gates = jnp.dot(conv_out, table_ref[...], preferred_element_type=jnp.float32)
    input_gate = jax.nn.sigmoid(gates[:, :channels] + gate_bias_ref[0:1, :])
    recur_gate = jax.nn.sigmoid(gates[:, channels:] + gate_bias_ref[1:2, :])
    param = decay_ref[...]
    softplus = jnp.maximum(param, 0.0) + jnp.log1p(jnp.exp(-jnp.abs(param)))
    log_decay = -8.0 * softplus * recur_gate
    decay = jnp.exp(log_decay)
    lost = -jnp.tanh(log_decay) * (decay * decay + 1.0)
    driven = jnp.sqrt(lost) * input_gate * conv_out.astype(jnp.float32)
    parts = channels // LANES
    for j in range(parts):
        a_ref[j] = decay[:, j * LANES : (j + 1) * LANES]
        b_ref[j] = driven[:, j * LANES : (j + 1) * LANES]

    lanes = 8
    length = rows // lanes

    def body(i, carry):
        at = pl.ds(i, lanes, stride=length)
        after = []
        for j in range(parts):
            product, state = carry[j]
            decay_now = a_ref[j, at, :]
            product = product * decay_now
            state = decay_now * state + b_ref[j, at, :]
            a_ref[j, at, :] = product
            b_ref[j, at, :] = state
            after.append((product, state))
        return tuple(after)

    fresh = (jnp.ones((lanes, LANES), jnp.float32), jnp.zeros((lanes, LANES), jnp.float32))
    totals = lax.fori_loop(0, length, body, (fresh,) * parts, unroll=8)
    for j in range(parts):
        product, state = totals[j]
        cols = slice(j * LANES, (j + 1) * LANES)
        start = jnp.zeros((1, LANES), jnp.float32)
        prefix = jnp.ones((1, LANES), jnp.float32)
        for i in range(lanes):
            at = pl.ds(i * length, length)
            within = a_ref[j, at, :]
            state_ref[at, cols] = b_ref[j, at, :] + within * start
            cumulative_ref[at, cols] = within * prefix
            start = product[i : i + 1, :] * start + state[i : i + 1, :]
            prefix = prefix * product[i : i + 1, :]
        end_ref[0:1, cols] = prefix
        end_ref[1:2, cols] = start


def local_scan(rec, before, conv_weight, conv_bias, table, gate_bias, decay_param):
    rows, inner = rec.shape
    width = table.shape[1] // 2
    lead = before.shape[0]

    def columns(height):
        return pl.BlockSpec((height, width), lambda h: (0, h))

    return pl.pallas_call(
        scan_kernel,
        grid=(inner // width,),
        out_shape=(
            jax.ShapeDtypeStruct((rows, inner), jnp.float32),
            jax.ShapeDtypeStruct((rows, inner), jnp.float32),
            jax.ShapeDtypeStruct((2, inner), jnp.float32),
        ),
        in_specs=[
            columns(rows), columns(lead), columns(conv_weight.shape[0]), columns(1),
            pl.BlockSpec((width, 2 * width), lambda h: (h, 0)), columns(2), columns(1),
        ],
        out_specs=(columns(rows), columns(rows), columns(2)),
        scratch_shapes=[
            pltpu.VMEM((rows + lead, width), jnp.float32),
            pltpu.VMEM((width // LANES, rows, LANES), jnp.float32),
            pltpu.VMEM((width // LANES, rows, LANES), jnp.float32),
        ],
    )(
        rec, before, conv_weight, conv_bias.reshape(1, inner), table, gate_bias,
        decay_param.reshape(1, inner),
    )


def shards(
    nz, paired, tokens, norm_gain, lru_proj, gelu_proj, conv_weight, conv_bias, gate_weights,
    gate_bias, decay_param,
):
    seq_count, tok_rows, width = tokens.shape
    inner = lru_proj.shape[1]
    taps = conv_weight.shape[0]
    if paired:
        out = fused_branch(
            nz, tokens.reshape(tok_rows, width), norm_gain, lru_proj, gelu_proj, conv_weight,
            conv_bias, gate_weights, gate_bias, decay_param,
        )
        return out.reshape(seq_count, tok_rows, inner)
    flat = tokens.reshape(tok_rows, width).astype(jnp.float32)
    mean_square = jnp.mean(flat * flat, axis=-1, keepdims=True)
    normed = (flat * lax.rsqrt(mean_square + 1e-06) * norm_gain).astype(jnp.bfloat16)
    every = [
        lax.all_gather(w, ("fsdp", "seq"), axis=0, tiled=True) for w in (lru_proj, gelu_proj)
    ]
    rec = jnp.dot(normed, every[0], preferred_element_type=jnp.float32).astype(jnp.bfloat16)
    act = jnp.dot(normed, every[1], preferred_element_type=jnp.float32)
    table = lax.all_gather(gate_weights, "seq", axis=0, tiled=True)
    lead = 8
    before = lax.ppermute(
        rec[tok_rows - lead :, :], "seq", [(i, i + 1) for i in range(nz - 1)]
    )
    local, cumulative, ends = local_scan(
        rec, before, conv_weight, conv_bias, table, gate_bias, decay_param
    )
    every_end = lax.all_gather(ends, "seq")
    position = lax.axis_index("seq")
    start = jnp.zeros((inner,), jnp.float32)
    for k in range(nz - 1):
        start = jnp.where(k < position, every_end[k, 0] * start + every_end[k, 1], start)
    gelu = jax.nn.gelu(act, approximate=True)
    out = ((local + cumulative * start) * gelu).astype(jnp.bfloat16)
    return out.reshape(seq_count, tok_rows, inner)


def solution(mesh):
    placed = (
        P("fsdp", "seq", None), P(), P(("fsdp", "seq"), None), P(("fsdp", "seq"), None), P(), P(),
        P("seq", None), P(), P(),
    )
    nz = mesh.shape["seq"]
    paired = mesh.shape["fsdp"] == 8 and 1 < nz <= 5
    return jax.shard_map(
        functools.partial(shards, nz, paired), mesh=mesh, in_specs=placed,
        out_specs=P("fsdp", "seq", None), check_vma=False,
    )
```

profile of v0, /device:TPU:25, one launch (start us, length us, event | category | flops | bytes accessed | tf_op | source)
XLA Modules:
  0.0 170.5 jit_solution(15586214968384202992)
XLA Ops:
  0.0 167.4 %shard_map.91 = bf16[512,2048]{1,0:T(8,128)(2,1)} custom-call(bf16[512,4096]{1,0:T(8,128)(2,1)} %bitcast.6, f32[1,4096]{1,0:T(1,128)} %bitcast.7, bf16[128,2048]{1,0:T(8,128)(2,1)} %lru_ref.1, bf16[128,2048]{1,0:T(8,128)(2,1)} %gelu_ref.1, bf16[512,512]{1,0:T(8,128)(2,1)} %gate_ref.1, f32[4,2048]{1,0:T(4,128)} %weight_ref.1, f32[1,2048]{1,0:T(1,128)} %bitcast.8, ...), custom_call_target="tpu_custom_call" | custom-call | tf_op jit(solution)/shard_map/pallas_call | solution.py:395
  167.4 3.2 %copy.11 = bf16[1,512,2048]{2,1,0:T(8,128)(2,1)} copy(bf16[1,512,2048]{2,1,0:T(8,128)(2,1)} %bitcast.5) | data formatting | bytes 4194304
where the time goes:
time: 174 us; the launch traced here: 171 us
  Pallas kernels  167 us (96%)
  local copies, waits for them, and re-layouts  3.16 us (2%)
    pallas_call x1, Pallas kernels, fused_branch(): pl.pallas_call(functools.partial(branch_kernel, nz), out_shape=jax.ShapeD...  167 us

commit v1 on v0

--- a/solution.py
+++ b/solution.py
@@ -12,18 +12,23 @@
 VMEM_BYTES = 66_000_000
 
 
-def normalise(tokens_ref, gain_ref, normed_ref, part, parts):
+def normalise(normed_ref, gain_ref, part, parts):
     rows = 32
 
     def body(i, _):
         at = pl.ds(pl.multiple_of(i * rows, rows), rows)
-        values = tokens_ref[at, :].astype(jnp.float32)
+        values = normed_ref[at, :].astype(jnp.float32)
         mean_square = jnp.mean(values * values, axis=-1, keepdims=True)
         normed_ref[at, :] = (values * lax.rsqrt(mean_square + 1e-06) * gain_ref[...]).astype(jnp.bfloat16)
         return 0
 
-    blocks = tokens_ref.shape[0] // rows // parts
+    blocks = normed_ref.shape[0] // rows // parts
     lax.fori_loop(part * blocks, (part + 1) * blocks, body, 0)
+
+
+LEAD = 4
+GAP = 2
+NORM_PARTS = 8
 
 
 def branch_kernel(
@@ -34,8 +39,8 @@
     w_ref, normed_ref, rec_ref, table_ref, before_ref, padded_ref, a_ref, b_ref,
     end_ref, carry_ref, start_ref,
     own_sem, send_sem, core_send, gate_send, gate_core_send, tail_send, carry_send,
-    z_recv, gate_recv, gate_core_recv, x_recv, y_recv, a_recv, b_recv, core_recv,
-    tail_recv, carry_recv,
+    z_recv, d_recv, gate_recv, gate_core_recv, x_own, y_own, x_rest, y_rest,
+    near_x, near_y, far_x, far_y, core_recv, tail_recv, carry_recv,
 ):
     f = lax.axis_index("fsdp")
     z = lax.axis_index("seq")
@@ -44,7 +49,7 @@
     fd = fx + 4 - 8 * y
     shard = lru_ref.shape[0]
     line = shard * nz
-    half = line // 2
+    half = shard // 2
     chunks = w_ref.shape[0]
     split = chunks // 2
     gate_rows = gate_ref.shape[0]
@@ -56,6 +61,9 @@
     pieces = channels // LANES
     taps = weight_ref.shape[0]
     lead = before_ref.shape[0]
+    last = nz - 1
+    reach = nz - 2
+    at_end = (z == 0) | (z == last)
 
     def remote(src, send, recv, device):
         return pltpu.make_async_remote_copy(
@@ -71,6 +79,8 @@
     own_gate = pl.ds(pl.multiple_of(z * gate_rows, gate_rows), gate_rows)
     gate_copy = pltpu.make_async_copy(gate_ref, table_ref.at[own_gate], own_sem.at[1])
     gate_copy.start()
+    token_copy = pltpu.make_async_copy(tokens_ref, normed_ref, own_sem.at[2])
+    token_copy.start()
 
     barrier = pltpu.get_barrier_semaphore()
     for device in ((fx, z), (fy, z), (fc, z)):
@@ -80,57 +90,71 @@
     def _():
         pl.semaphore_signal(barrier, inc=1, device_id=(f, z - 1), device_id_type=MESH)
 
-    @pl.when(z < nz - 1)
+    @pl.when(z < last)
     def _():
         pl.semaphore_signal(barrier, inc=1, device_id=(f, z + 1), device_id_type=MESH)
 
     for k in range(nz):
         @pl.when(z == k)
         def _():
-            pl.semaphore_wait(barrier, 3 + int(k > 0) + int(k < nz - 1))
+            pl.semaphore_wait(barrier, 3 + int(k > 0) + int(k < last))
 
     pltpu.make_async_copy(w_ref.at[:, own], w_ref.at[:, own], own_sem.at[0]).wait()
     gate_copy.wait()
 
-    def shard_of(t, source):
-        at = pl.ds(pl.multiple_of((f * nz + source) * shard, shard), shard)
-        return w_ref.at[t, at]
+    def unit(t, owner, k, first=0, size=shard):
+        start = (owner * nz + k) * shard + first
+        return w_ref.at[t, pl.ds(pl.multiple_of(start, half), size)]
+
+    def whole_line(t, owner):
+        return w_ref.at[t, pl.ds(pl.multiple_of(owner * line, line), line)]
 
     def gate_of(t, source):
         first = source * gate_rows + c * (gate_rows // 2) + t * piece
         return table_ref.at[pl.ds(pl.multiple_of(first, piece), piece)]
 
-    def pass_on(t, source, target):
-        remote(shard_of(t, source), send_sem.at[t], z_recv.at[t, source], (f, target)).start()
+    def along_z(t, k, target):
+        remote(unit(t, f, k), send_sem.at[t], z_recv.at[t, k], (f, target)).start()
 
         @pl.when(t < gate_steps)
         def _():
-            remote(gate_of(t, source), gate_send.at[t], gate_recv.at[t, source], (f, target)).start()
-
-    def arrived(t, source):
-        remote(shard_of(t, source), send_sem.at[t], z_recv.at[t, source], (f, z)).wait_recv()
+            remote(gate_of(t, k), gate_send.at[t], gate_recv.at[t, k], (f, target)).start()
+
+    def across(t, k, recv_x, recv_y):
+        remote(unit(t, f, k), send_sem.at[t], recv_x.at[t], (fx, z)).start()
+        remote(unit(t, f, k), send_sem.at[t], recv_y.at[t], (fy, z)).start()
+
+    def diagonal(t, k, target):
+        remote(unit(t, fd, k), send_sem.at[t], d_recv.at[t, k], (f, target)).start()
+
+    def arrived(t, k):
+        remote(unit(t, f, k), send_sem.at[t], z_recv.at[t, k], (f, z)).wait_recv()
 
         @pl.when(t < gate_steps)
         def _():
-            remote(gate_of(t, source), gate_send.at[t], gate_recv.at[t, source], (f, z)).wait_recv()
-
-    def z_first(t):
+            remote(gate_of(t, k), gate_send.at[t], gate_recv.at[t, k], (f, z)).wait_recv()
+
+    def own_first(t):
         @pl.when(z > 0)
         def _():
-            pass_on(t, z, z - 1)
-
-        @pl.when(z < nz - 1)
-        def _():
-            pass_on(t, z, z + 1)
+            along_z(t, z, z - 1)
+
+        @pl.when(z < last)
+        def _():
+            along_z(t, z, z + 1)
+
+        across(t, z, x_own, y_own)
 
     def z_hop(t, distance):
         @pl.when(z >= distance)
         def _():
             arrived(t, z - distance)
 
-            @pl.when(z < nz - 1)
+            @pl.when(z < last)
             def _():
-                pass_on(t, z - distance, z + 1)
+                along_z(t, z - distance, z + 1)
+
+            across(t, z - distance, x_rest, y_rest)
 
         @pl.when(z + distance < nz)
         def _():
@@ -138,50 +162,99 @@
 
             @pl.when(z > 0)
             def _():
-                pass_on(t, z + distance, z - 1)
-
-    def rows_of(owner, t, start, size):
-        return w_ref.at[t, pl.ds(pl.multiple_of(owner * line + start, shard), size)]
-
-    def to_core(t, owner, start, size):
-        remote(rows_of(owner, t, start, size), core_send.at[t], core_recv.at[t], (fc, z)).start()
+                along_z(t, z + distance, z - 1)
+
+            across(t, z + distance, x_rest, y_rest)
 
     def line_done(t):
-        mine = rows_of(f, t, 0, line)
-        remote(mine, send_sem.at[t], x_recv.at[t], (fx, z)).start()
-        remote(mine, send_sem.at[t], y_recv.at[t], (fy, z)).start()
-        to_core(t, f, 0, line)
+        remote(whole_line(t, f), core_send.at[t], core_recv.at[t], (fc, z)).start()
 
         @pl.when(t < gate_steps)
         def _():
-            for source in range(nz):
-                @pl.when(z != source)
+            for k in range(nz):
+                @pl.when(z != k)
                 def _():
-                    remote(
-                        gate_of(t, source), gate_core_send.at[t], gate_core_recv.at[t], (fc, z)
-                    ).start()
+                    remote(gate_of(t, k), gate_core_send.at[t], gate_core_recv.at[t], (fc, z)).start()
 
     def gate_done(t):
         @pl.when(t < gate_steps)
         def _():
-            others = table_ref.at[pl.ds(0, (nz - 1) * piece)]
+            others = table_ref.at[pl.ds(0, last * piece)]
             pltpu.make_async_copy(others, others, gate_core_recv.at[t]).wait()
 
-    def sides_done(t):
-        from_x = rows_of(fx, t, 0, line)
-        remote(from_x, send_sem.at[t], x_recv.at[t], (fx, z)).wait_recv()
-        remote(rows_of(fx, t, 0, half), send_sem.at[t], a_recv.at[t], (fy, z)).start()
-        to_core(t, fx, 0, line)
-        from_y = rows_of(fy, t, 0, line)
-        remote(from_y, send_sem.at[t], y_recv.at[t], (fy, z)).wait_recv()
-        remote(rows_of(fy, t, half, half), send_sem.at[t], b_recv.at[t], (fx, z)).start()
-        to_core(t, fy, 0, line)
+    def plane(t):
+        remote(unit(t, fx, z), send_sem.at[t], x_own.at[t], (fx, z)).wait_recv()
+        remote(unit(t, fx, z, 0, half), send_sem.at[t], near_y.at[t], (fy, z)).start()
+        remote(unit(t, fy, z), send_sem.at[t], y_own.at[t], (fy, z)).wait_recv()
+        remote(unit(t, fy, z, half, half), send_sem.at[t], near_x.at[t], (fx, z)).start()
+
+    def corner(t):
+        remote(unit(t, fd, z, 0, half), send_sem.at[t], near_y.at[t], (fy, z)).wait_recv()
+        remote(unit(t, fd, z, half, half), send_sem.at[t], near_x.at[t], (fx, z)).wait_recv()
+
+        @pl.when(z > 0)
+        def _():
+            diagonal(t, z, z - 1)
+
+        @pl.when(z < last)
+        def _():
+            diagonal(t, z, z + 1)
+
+    def d_hop(t, distance):
+        free = (t >= split) | (distance < reach)
+        onward = (t >= split) | (distance + 1 < reach)
+
+        @pl.when((z >= distance) & (free | (z < last)))
+        def _():
+            remote(unit(t, fd, z - distance), send_sem.at[t], d_recv.at[t, z - distance], (f, z)).wait_recv()
+
+            if distance < reach:
+                @pl.when((z < last) & (onward | (z + 1 < last)))
+                def _():
+                    diagonal(t, z - distance, z + 1)
+
+        @pl.when((z + distance < nz) & (free | (z > 0)))
+        def _():
+            remote(unit(t, fd, z + distance), send_sem.at[t], d_recv.at[t, z + distance], (f, z)).wait_recv()
+
+            if distance < reach:
+                @pl.when((z > 0) & (onward | (z - 1 > 0)))
+                def _():
+                    diagonal(t, z + distance, z - 1)
+
+    far = last - z
+    middle = jnp.where(z == 0, reach, 1)
+
+    def sides(t):
+        rest = w_ref.at[t, pl.ds(0, last * shard)]
+        remote(rest, send_sem.at[t], x_rest.at[t], (fx, z)).wait_recv()
+        remote(rest, send_sem.at[t], y_rest.at[t], (fy, z)).wait_recv()
+
+        @pl.when(at_end & (t < split))
+        def _():
+            remote(unit(t, fx, far), send_sem.at[t], far_y.at[t], (fy, z)).start()
+            remote(unit(t, fy, middle), send_sem.at[t], far_x.at[t], (fx, z)).start()
+
+        @pl.when(at_end & (t >= split))
+        def _():
+            remote(unit(t, fx, far, 0, half), send_sem.at[t], far_y.at[t], (fy, z)).start()
+            remote(unit(t, fy, far, half, half), send_sem.at[t], far_x.at[t], (fx, z)).start()
+
+        remote(whole_line(t, fx), core_send.at[t], core_recv.at[t], (fc, z)).start()
+        remote(whole_line(t, fy), core_send.at[t], core_recv.at[t], (fc, z)).start()
 
     def corner_done(t):
-        remote(rows_of(fd, t, 0, half), send_sem.at[t], a_recv.at[t], (fy, z)).wait_recv()
-        to_core(t, fd, 0, half)
-        remote(rows_of(fd, t, half, half), send_sem.at[t], b_recv.at[t], (fx, z)).wait_recv()
-        to_core(t, fd, half, half)
+        @pl.when(at_end & (t < split))
+        def _():
+            remote(unit(t, fd, far), send_sem.at[t], far_y.at[t], (fy, z)).wait_recv()
+            remote(unit(t, fd, middle), send_sem.at[t], far_x.at[t], (fx, z)).wait_recv()
+
+        @pl.when(at_end & (t >= split))
+        def _():
+            remote(unit(t, fd, far, 0, half), send_sem.at[t], far_y.at[t], (fy, z)).wait_recv()
+            remote(unit(t, fd, far, half, half), send_sem.at[t], far_x.at[t], (fx, z)).wait_recv()
+
+        remote(whole_line(t, fd), core_send.at[t], core_recv.at[t], (fc, z)).start()
 
     def multiply(t):
         whole = w_ref.at[t, pl.ds(0, 4 * line)]
@@ -226,7 +299,7 @@
         )
 
     def send_tail(h):
-        @pl.when(z < nz - 1)
+        @pl.when(z < last)
         def _():
             tail_copy(h, rows - lead, (f, z + 1)).start()
 
@@ -295,13 +368,13 @@
         def _():
             carry_copy(h, (f, z)).wait_recv()
 
-        @pl.when(z < nz - 1)
+        @pl.when(z < last)
         def _():
             end = end_ref[0:1, cols] * start_ref[0:1, cols] + end_ref[1:2, cols]
             carry_ref[:, cols] = jnp.broadcast_to(end, (carry_ref.shape[0], channels))
 
     def send_carry(h):
-        @pl.when(z < nz - 1)
+        @pl.when(z < last)
         def _():
             carry_copy(h, (f, z + 1)).start()
 
@@ -310,12 +383,22 @@
         before_ref[...] = jnp.zeros_like(before_ref)
         start_ref[...] = jnp.zeros_like(start_ref)
 
-    stages = [z_first]
+    stages = []
     for distance in range(1, nz):
-        stages.append(functools.partial(z_hop, distance=distance))
-    stages += [line_done, sides_done, corner_done, gate_done, multiply]
-    lags = list(range(nz)) + [nz - 1, nz, nz + 1, nz + 1, nz + 2]
-    scan_at = gate_steps + nz
+        stages.append((functools.partial(z_hop, distance=distance), LEAD + GAP * (distance - 1)))
+    stages += [(plane, LEAD), (corner, LEAD + GAP)]
+    for distance in range(1, nz - 1):
+        stages.append((functools.partial(d_hop, distance=distance), LEAD + GAP * (distance + 1)))
+    line_lag = LEAD + GAP * (nz - 2)
+    sides_lag = line_lag + GAP
+    stages += [
+        (line_done, line_lag), (gate_done, line_lag + 1),
+        (sides, sides_lag), (corner_done, sides_lag + GAP), (own_first, 0),
+    ]
+    finish = sides_lag + GAP + 1
+    tail_at = finish + pieces
+    scan_at = max(tail_at + 2, line_lag + gate_steps)
+    steps = chunks + finish
 
     def on_head(s, first, stage):
         @pl.when((s >= first) & (s < first + pieces * heads) & ((s - first) % pieces == 0))
@@ -323,41 +406,63 @@
             stage((s - first) // pieces)
 
     def step(s, _):
-        for stage, lag in zip(stages[:-1], lags[:-1]):
+        for stage, lag in stages:
             @pl.when((s >= lag) & (s < chunks + lag))
             def _():
                 stage(s - lag)
 
         on_head(s, scan_at + 2 + 2 * z, send_carry)
-        on_head(s, nz + 2 + pieces, send_tail)
-
-        @pl.when(s < 4)
-        def _():
-            normalise(tokens_ref, gain_ref, normed_ref, s, 4)
+        on_head(s, tail_at, send_tail)
+
+        @pl.when(s == LEAD)
+        def _():
+            token_copy.wait()
+
+        @pl.when((s >= LEAD) & (s < LEAD + NORM_PARTS))
+        def _():
+            normalise(normed_ref, gain_ref, s - LEAD, NORM_PARTS)
 
         on_head(s, scan_at + 1 + 2 * z, make_carry)
 
-        @pl.when((s >= lags[-1]) & (s < chunks + lags[-1]))
-        def _():
-            multiply(s - lags[-1])
+        @pl.when((s >= finish) & (s < chunks + finish))
+        def _():
+            multiply(s - finish)
 
         on_head(s, scan_at, scan)
         return 0
 
-    lax.fori_loop(0, chunks + lags[-1], step, 0)
+    lax.fori_loop(0, steps, step, 0)
+
+    def units_sent(k, early):
+        count = 2 + 2 * last + 1 + 2 * (int(k > 0) + int(k < last))
+        for distance in range(1, nz):
+            count += int(k >= distance and k < last) + int(k + distance < nz and k > 0)
+            if distance < reach:
+                open_up = not early or distance + 1 < reach or k + 1 < last
+                open_down = not early or distance + 1 < reach or k - 1 > 0
+                count += int(k >= distance and k < last and open_up)
+                count += int(k + distance < nz and k > 0 and open_down)
+        if k == 0 or k == last:
+            count += 2 if early else 1
+        return count
 
     def drain(t, _):
         for k in range(nz):
-            shards_sent = (k + 1 if k < nz - 1 else 0) + (nz - k if k > 0 else 0)
+            passed = int(k > 0) + int(k < last)
+            for distance in range(1, nz):
+                passed += int(k >= distance and k < last) + int(k + distance < nz and k > 0)
 
             @pl.when(z == k)
             def _():
-                sent = w_ref.at[t, pl.ds(0, shards_sent * shard + 3 * line)]
-                pltpu.make_async_copy(sent, sent, send_sem.at[t]).wait()
+                for early in (True, False):
+                    @pl.when((t < split) if early else (t >= split))
+                    def _():
+                        sent = w_ref.at[t, pl.ds(0, units_sent(k, early) * shard)]
+                        pltpu.make_async_copy(sent, sent, send_sem.at[t]).wait()
 
                 @pl.when(t < gate_steps)
                 def _():
-                    sent_gate = table_ref.at[pl.ds(0, shards_sent * piece)]
+                    sent_gate = table_ref.at[pl.ds(0, passed * piece)]
                     pltpu.make_async_copy(sent_gate, sent_gate, gate_send.at[t]).wait()
 
         whole = w_ref.at[t, pl.ds(0, 4 * line)]
@@ -365,10 +470,10 @@
 
         @pl.when(t < gate_steps)
         def _():
-            others = table_ref.at[pl.ds(0, (nz - 1) * piece)]
+            others = table_ref.at[pl.ds(0, last * piece)]
             pltpu.make_async_copy(others, others, gate_core_send.at[t]).wait()
 
-        @pl.when((t < heads) & (z < nz - 1))
+        @pl.when((t < heads) & (z < last))
         def _():
             tail_copy(t, rows - lead, (f, z)).wait_send()
             carry_copy(t, (f, z)).wait_send()
@@ -392,10 +497,11 @@
     dma = pltpu.SemaphoreType.DMA
     f32, bf16 = jnp.float32, jnp.bfloat16
     lead = 16
+    each = dma((chunks,))
     return pl.pallas_call(
         functools.partial(branch_kernel, nz),
         out_shape=jax.ShapeDtypeStruct((rows, inner), bf16),
-        in_specs=[vmem, vmem, any_, any_, any_, vmem, vmem, vmem, vmem],
+        in_specs=[any_, vmem, any_, any_, any_, vmem, vmem, vmem, vmem],
         out_specs=vmem,
         scratch_shapes=[
             pltpu.VMEM((chunks, width, LANES), bf16),
@@ -407,10 +513,10 @@
             pltpu.VMEM((chunks // 2, rows, LANES), f32),
             pltpu.VMEM((chunks // 2, rows, LANES), f32),
             pltpu.VMEM((8, inner), f32), pltpu.VMEM((8, inner), f32), pltpu.VMEM((8, inner), f32),
-            dma((2,)), dma((chunks,)), dma((chunks,)), dma((chunks // 4,)), dma((chunks // 4,)),
+            dma((3,)), each, each, dma((chunks // 4,)), dma((chunks // 4,)),
             dma((heads,)), dma((heads,)),
-            dma((chunks, nz)), dma((chunks // 4, nz)), dma((chunks // 4,)),
-            dma((chunks,)), dma((chunks,)), dma((chunks,)), dma((chunks,)), dma((chunks,)),
+            dma((chunks, nz)), dma((chunks, nz)), dma((chunks // 4, nz)), dma((chunks // 4,)),
+            each, each, each, each, each, each, each, each, each,
             dma((heads,)), dma((heads,)),
         ],
         compiler_params=pltpu.CompilerParams(
@@ -560,7 +666,7 @@
         P("seq", None), P(), P(),
     )
     nz = mesh.shape["seq"]
-    paired = mesh.shape["fsdp"] == 8 and 1 < nz <= 5
+    paired = mesh.shape["fsdp"] == 8 and 3 < nz <= 5
     return jax.shard_map(
         functools.partial(shards, nz, paired), mesh=mesh, in_specs=placed,
         out_specs=P("fsdp", "seq", None), check_vma=False,

time: 174 us -> 152 us (0.87)
  Pallas kernels: 167 us -> 146 us
    pallas_call x1, Pallas kernels: 167 us -> 146 us  [fused_branch(): pl.pallas_call(functools.partial(branch_kernel, nz), out_shape=jax.ShapeD...]
where the time goes in v1:
time: 152 us; the launch traced here: 149 us
  Pallas kernels  146 us (96%)
  local copies, waits for them, and re-layouts  3.16 us (2%)
    pallas_call x1, Pallas kernels, fused_branch(): pl.pallas_call(functools.partial(branch_kernel, nz), out_shape=jax.ShapeD...  146 us
    unnamed x1, local copies, waits for them, and re-layouts  3.16 us

profile of v1, /device:TPU:25, one launch (start us, length us, event | category | flops | bytes accessed | tf_op | source)
XLA Modules:
  0.0 149.2 jit_solution(11773160284314777838)
XLA Ops:
  0.0 146.0 %shard_map.91 = bf16[512,2048]{1,0:T(8,128)(2,1)} custom-call(bf16[512,4096]{1,0:T(8,128)(2,1)} %bitcast.6, f32[1,4096]{1,0:T(1,128)} %bitcast.7, bf16[128,2048]{1,0:T(8,128)(2,1)} %lru_ref.1, bf16[128,2048]{1,0:T(8,128)(2,1)} %gelu_ref.1, bf16[512,512]{1,0:T(8,128)(2,1)} %gate_ref.1, f32[4,2048]{1,0:T(4,128)} %weight_ref.1, f32[1,2048]{1,0:T(1,128)} %bitcast.8, ...), custom_call_target="tpu_custom_call" | custom-call | tf_op jit(solution)/shard_map/pallas_call | solution.py:501
  146.0 3.2 %copy.11 = bf16[1,512,2048]{2,1,0:T(8,128)(2,1)} copy(bf16[1,512,2048]{2,1,0:T(8,128)(2,1)} %bitcast.5) | data formatting | bytes 4194304

commit v2 on v0

--- a/solution.py
+++ b/solution.py
@@ -12,30 +12,68 @@
 VMEM_BYTES = 66_000_000
 
 
-def normalise(tokens_ref, gain_ref, normed_ref, part, parts):
+def normalise(normed_ref, gain_ref, part, parts):
     rows = 32
 
     def body(i, _):
         at = pl.ds(pl.multiple_of(i * rows, rows), rows)
-        values = tokens_ref[at, :].astype(jnp.float32)
+        values = normed_ref[at, :].astype(jnp.float32)
         mean_square = jnp.mean(values * values, axis=-1, keepdims=True)
         normed_ref[at, :] = (values * lax.rsqrt(mean_square + 1e-06) * gain_ref[...]).astype(jnp.bfloat16)
         return 0
 
-    blocks = tokens_ref.shape[0] // rows // parts
+    blocks = normed_ref.shape[0] // rows // parts
     lax.fori_loop(part * blocks, (part + 1) * blocks, body, 0)
+
+
+LEAD = 4
+GAP = 2
+NORM_PARTS = 4
+TALL = 512
+
+
+def hop_counts(nz, k, early, gates):
+    last, reach = nz - 1, nz - 2
+    twice = 2 if gates else 1
+    end = k in (0, last)
+    got = {0: 2, 1: 1}
+    for distance in range(1, nz):
+        sources = int(k >= distance) + int(k + distance < nz)
+        got[distance - 1] = got.get(distance - 1, 0) + twice * sources
+        if distance <= reach:
+            for source in (k - distance, k + distance):
+                if 0 <= source < nz and not (early and end and distance == reach):
+                    got[distance + 1] = got.get(distance + 1, 0) + 1
+    got[last] = got.get(last, 0) + 2 * last
+    far = (2 if early else 1) if end else 0
+    sent = 2 + 2 * last + 1 + far
+    for source in range(nz):
+        for target in (k - 1, k + 1):
+            onward = (target - k) * (k - source) >= 0
+            if not (0 <= target < nz and onward):
+                continue
+            sent += 1
+            distance = abs(target - source)
+            closed = early and target in (0, last) and distance == reach
+            if distance <= reach and not closed:
+                sent += 1
+    passed = sum(
+        1 for source in range(nz) for target in (k - 1, k + 1)
+        if 0 <= target < nz and (target - k) * (k - source) >= 0
+    )
+    return got, far, sent, passed
 
 
 def branch_kernel(
     nz,
-    tokens_ref, gain_ref, lru_ref, gelu_ref, gate_ref,
-    weight_ref, bias_ref, gate_bias_ref, decay_ref,
-    out_ref,
+    tokens_ref, gain_in, lru_ref, gelu_ref, gate_ref,
+    weight_in, bias_in, gate_bias_in, decay_in,
+    result_ref,
+    gain_ref, weight_ref, bias_ref, gate_bias_ref, decay_ref, out_ref,
     w_ref, normed_ref, rec_ref, table_ref, before_ref, padded_ref, a_ref, b_ref,
     end_ref, carry_ref, start_ref,
-    own_sem, send_sem, core_send, gate_send, gate_core_send, tail_send, carry_send,
-    z_recv, gate_recv, gate_core_recv, x_recv, y_recv, a_recv, b_recv, core_recv,
-    tail_recv, carry_recv,
+    own_sem, out_sem, send_sem, core_send, gate_send, gate_core_send, tail_send, carry_send,
+    hop_recv, far_recv, core_recv, gate_core_recv, tail_recv, carry_recv,
 ):
     f = lax.axis_index("fsdp")
     z = lax.axis_index("seq")
@@ -44,8 +82,8 @@
     fd = fx + 4 - 8 * y
     shard = lru_ref.shape[0]
     line = shard * nz
-    half = line // 2
-    chunks = w_ref.shape[0]
+    half = shard // 2
+    chunks, _, wide = w_ref.shape
     split = chunks // 2
     gate_rows = gate_ref.shape[0]
     gate_steps = split // 2
@@ -56,6 +94,9 @@
     pieces = channels // LANES
     taps = weight_ref.shape[0]
     lead = before_ref.shape[0]
+    last = nz - 1
+    reach = nz - 2
+    at_end = (z == 0) | (z == last)
 
     def remote(src, send, recv, device):
         return pltpu.make_async_remote_copy(
@@ -66,11 +107,22 @@
     own = pl.ds(pl.multiple_of((f * nz + z) * shard, shard), shard)
     for t in range(chunks):
         src = lru_ref if t < split else gelu_ref
-        cols = pl.ds((t % split) * LANES, LANES)
+        cols = pl.ds((t % split) * wide, wide)
         pltpu.make_async_copy(src.at[:, cols], w_ref.at[t, own], own_sem.at[0]).start()
     own_gate = pl.ds(pl.multiple_of(z * gate_rows, gate_rows), gate_rows)
     gate_copy = pltpu.make_async_copy(gate_ref, table_ref.at[own_gate], own_sem.at[1])
     gate_copy.start()
+    token_copy = pltpu.make_async_copy(tokens_ref, normed_ref, own_sem.at[2])
+    token_copy.start()
+    small = [
+        pltpu.make_async_copy(source, target, own_sem.at[3 + i])
+        for i, (source, target) in enumerate((
+            (gain_in, gain_ref), (weight_in, weight_ref), (bias_in, bias_ref),
+            (gate_bias_in, gate_bias_ref), (decay_in, decay_ref),
+        ))
+    ]
+    for copy in small:
+        copy.start()
 
     barrier = pltpu.get_barrier_semaphore()
     for device in ((fx, z), (fy, z), (fc, z)):
@@ -80,117 +132,184 @@
     def _():
         pl.semaphore_signal(barrier, inc=1, device_id=(f, z - 1), device_id_type=MESH)
 
-    @pl.when(z < nz - 1)
+    @pl.when(z < last)
     def _():
         pl.semaphore_signal(barrier, inc=1, device_id=(f, z + 1), device_id_type=MESH)
 
     for k in range(nz):
         @pl.when(z == k)
         def _():
-            pl.semaphore_wait(barrier, 3 + int(k > 0) + int(k < nz - 1))
+            pl.semaphore_wait(barrier, 3 + int(k > 0) + int(k < last))
 
     pltpu.make_async_copy(w_ref.at[:, own], w_ref.at[:, own], own_sem.at[0]).wait()
     gate_copy.wait()
 
-    def shard_of(t, source):
-        at = pl.ds(pl.multiple_of((f * nz + source) * shard, shard), shard)
-        return w_ref.at[t, at]
+    def unit(t, owner, k, first=0, size=shard):
+        start = (owner * nz + k) * shard + first
+        return w_ref.at[t, pl.ds(pl.multiple_of(start, half), size)]
+
+    def whole_line(t, owner):
+        return w_ref.at[t, pl.ds(pl.multiple_of(owner * line, line), line)]
 
     def gate_of(t, source):
         first = source * gate_rows + c * (gate_rows // 2) + t * piece
         return table_ref.at[pl.ds(pl.multiple_of(first, piece), piece)]
 
-    def pass_on(t, source, target):
-        remote(shard_of(t, source), send_sem.at[t], z_recv.at[t, source], (f, target)).start()
+    send, core = send_sem.at[0], core_send.at[0]
+
+    def along_z(t, k, target, distance):
+        remote(unit(t, f, k), send, hop_recv.at[t, distance - 1], (f, target)).start()
 
         @pl.when(t < gate_steps)
         def _():
-            remote(gate_of(t, source), gate_send.at[t], gate_recv.at[t, source], (f, target)).start()
-
-    def arrived(t, source):
-        remote(shard_of(t, source), send_sem.at[t], z_recv.at[t, source], (f, z)).wait_recv()
-
-        @pl.when(t < gate_steps)
-        def _():
-            remote(gate_of(t, source), gate_send.at[t], gate_recv.at[t, source], (f, z)).wait_recv()
-
-    def z_first(t):
+            remote(gate_of(t, k), gate_send.at[0], hop_recv.at[t, distance - 1], (f, target)).start()
+
+    def across(t, k, hop):
+        remote(unit(t, f, k), send, hop_recv.at[t, hop], (fx, z)).start()
+        remote(unit(t, f, k), send, hop_recv.at[t, hop], (fy, z)).start()
+
+    def diagonal(t, k, target, distance):
+        remote(unit(t, fd, k), send, hop_recv.at[t, distance + 1], (f, target)).start()
+
+    def wait_hop(t, hop):
+        sizes = {}
+        for k in range(nz):
+            for early, gates in ((True, True), (True, False), (False, False)):
+                count = hop_counts(nz, k, early, gates)[0].get(hop, 0)
+                sizes.setdefault(count, {}).setdefault((early, gates), []).append(k)
+        for count, places in sizes.items():
+            if count == 0:
+                continue
+            chosen = False
+            for (early, gates), ks in places.items():
+                when = (t < gate_steps) if gates else ((t >= gate_steps) & (t < split)) if early else (t >= split)
+                if len(ks) < nz:
+                    there = z == ks[0]
+                    for k in ks[1:]:
+                        there = there | (z == k)
+                    when = when & there
+                chosen = when if chosen is False else chosen | when
+
+            @pl.when(chosen)
+            def _():
+                block = w_ref.at[0, pl.ds(0, count * shard)]
+                pltpu.make_async_copy(block, block, hop_recv.at[t, hop]).wait()
+
+    def own_first(t):
         @pl.when(z > 0)
         def _():
-            pass_on(t, z, z - 1)
-
-        @pl.when(z < nz - 1)
-        def _():
-            pass_on(t, z, z + 1)
+            along_z(t, z, z - 1, 1)
+
+        @pl.when(z < last)
+        def _():
+            along_z(t, z, z + 1, 1)
+
+        across(t, z, 0)
 
     def z_hop(t, distance):
+        @pl.when((z >= distance) & (z < last))
+        def _():
+            along_z(t, z - distance, z + 1, distance + 1)
+
+        @pl.when((z + distance < nz) & (z > 0))
+        def _():
+            along_z(t, z + distance, z - 1, distance + 1)
+
+    def sideways(t, distance):
         @pl.when(z >= distance)
         def _():
-            arrived(t, z - distance)
-
-            @pl.when(z < nz - 1)
-            def _():
-                pass_on(t, z - distance, z + 1)
+            across(t, z - distance, last)
 
         @pl.when(z + distance < nz)
         def _():
-            arrived(t, z + distance)
-
+            across(t, z + distance, last)
+
+    def d_hop(t, distance):
+        onward = (t >= split) | (distance + 1 < reach)
+
+        @pl.when((z >= distance) & (z < last) & (onward | (z + 1 < last)))
+        def _():
+            diagonal(t, z - distance, z + 1, distance + 1)
+
+        @pl.when((z + distance < nz) & (z > 0) & (onward | (z - 1 > 0)))
+        def _():
+            diagonal(t, z + distance, z - 1, distance + 1)
+
+    far = last - z
+    middle = jnp.where(z == 0, reach, 1)
+
+    def hop_done(t, hop):
+        wait_hop(t, hop)
+        if hop + 1 < last:
+            z_hop(t, hop + 1)
+        if hop == 0:
+            remote(unit(t, fx, z, 0, half), send, hop_recv.at[t, 1], (fy, z)).start()
+            remote(unit(t, fy, z, half, half), send, hop_recv.at[t, 1], (fx, z)).start()
+        if hop == 1:
             @pl.when(z > 0)
             def _():
-                pass_on(t, z + distance, z - 1)
-
-    def rows_of(owner, t, start, size):
-        return w_ref.at[t, pl.ds(pl.multiple_of(owner * line + start, shard), size)]
-
-    def to_core(t, owner, start, size):
-        remote(rows_of(owner, t, start, size), core_send.at[t], core_recv.at[t], (fc, z)).start()
-
-    def line_done(t):
-        mine = rows_of(f, t, 0, line)
-        remote(mine, send_sem.at[t], x_recv.at[t], (fx, z)).start()
-        remote(mine, send_sem.at[t], y_recv.at[t], (fy, z)).start()
-        to_core(t, f, 0, line)
-
-        @pl.when(t < gate_steps)
-        def _():
-            for source in range(nz):
-                @pl.when(z != source)
-                def _():
-                    remote(
-                        gate_of(t, source), gate_core_send.at[t], gate_core_recv.at[t], (fc, z)
-                    ).start()
+                diagonal(t, z, z - 1, 1)
+
+            @pl.when(z < last)
+            def _():
+                diagonal(t, z, z + 1, 1)
+        if 2 <= hop < last:
+            d_hop(t, hop - 1)
+        if hop + 1 <= last:
+            sideways(t, hop + 1)
+        if hop + 1 == last:
+            remote(whole_line(t, f), core, core_recv.at[t], (fc, z)).start()
+
+            @pl.when(t < gate_steps)
+            def _():
+                for k in range(nz):
+                    @pl.when(z != k)
+                    def _():
+                        remote(gate_of(t, k), gate_core_send.at[0], gate_core_recv.at[t], (fc, z)).start()
+        if hop == last:
+            @pl.when(at_end & (t < split))
+            def _():
+                remote(unit(t, fx, far), send, far_recv.at[t], (fy, z)).start()
+                remote(unit(t, fy, middle), send, far_recv.at[t], (fx, z)).start()
+
+            @pl.when(at_end & (t >= split))
+            def _():
+                remote(unit(t, fx, far, 0, half), send, far_recv.at[t], (fy, z)).start()
+                remote(unit(t, fy, far, half, half), send, far_recv.at[t], (fx, z)).start()
+
+            remote(whole_line(t, fx), core, core_recv.at[t], (fc, z)).start()
+            remote(whole_line(t, fy), core, core_recv.at[t], (fc, z)).start()
 
     def gate_done(t):
         @pl.when(t < gate_steps)
         def _():
-            others = table_ref.at[pl.ds(0, (nz - 1) * piece)]
+            others = table_ref.at[pl.ds(0, last * piece)]
             pltpu.make_async_copy(others, others, gate_core_recv.at[t]).wait()
 
-    def sides_done(t):
-        from_x = rows_of(fx, t, 0, line)
-        remote(from_x, send_sem.at[t], x_recv.at[t], (fx, z)).wait_recv()
-        remote(rows_of(fx, t, 0, half), send_sem.at[t], a_recv.at[t], (fy, z)).start()
-        to_core(t, fx, 0, line)
-        from_y = rows_of(fy, t, 0, line)
-        remote(from_y, send_sem.at[t], y_recv.at[t], (fy, z)).wait_recv()
-        remote(rows_of(fy, t, half, half), send_sem.at[t], b_recv.at[t], (fx, z)).start()
-        to_core(t, fy, 0, line)
-
     def corner_done(t):
-        remote(rows_of(fd, t, 0, half), send_sem.at[t], a_recv.at[t], (fy, z)).wait_recv()
-        to_core(t, fd, 0, half)
-        remote(rows_of(fd, t, half, half), send_sem.at[t], b_recv.at[t], (fx, z)).wait_recv()
-        to_core(t, fd, half, half)
+        @pl.when(at_end & (t < split))
+        def _():
+            block = w_ref.at[0, pl.ds(0, 2 * shard)]
+            pltpu.make_async_copy(block, block, far_recv.at[t]).wait()
+
+        @pl.when(at_end & (t >= split))
+        def _():
+            block = w_ref.at[0, pl.ds(0, shard)]
+            pltpu.make_async_copy(block, block, far_recv.at[t]).wait()
+
+        remote(whole_line(t, fd), core, core_recv.at[t], (fc, z)).start()
+
+    def put_out(h):
+        return pltpu.make_async_copy(out_ref.at[:, columns(h)], result_ref.at[:, columns(h)], out_sem.at[0])
 
     def multiply(t):
         whole = w_ref.at[t, pl.ds(0, 4 * line)]
         pltpu.make_async_copy(whole, whole, core_recv.at[t]).wait()
-        blocks = normed_ref.shape[0] // 512
-        column = pl.ds(pl.multiple_of((t % split) * LANES, LANES), LANES)
+        column = columns(t % split)
+        tall = TALL
 
         def body(i, _):
-            at = pl.ds(pl.multiple_of(i * 512, 512), 512)
+            at = pl.ds(pl.multiple_of(i * tall, tall), tall)
             product = jnp.dot(normed_ref[at, :], w_ref[t], preferred_element_type=jnp.float32)
 
             @pl.when(t < split)
@@ -199,13 +318,20 @@
 
             @pl.when(t >= split)
             def _():
-                chunk = jnp.maximum(t - split, 0)
-                state = b_ref[chunk, at, :] + a_ref[chunk, at, :] * start_ref[0:1, column]
-                out_ref[at, column] = (state * jax.nn.gelu(product, approximate=True)).astype(out_ref.dtype)
+                h = jnp.maximum(t - split, 0)
+                for j in range(pieces):
+                    lanes = pl.ds(pl.multiple_of(h * channels + j * LANES, LANES), LANES)
+                    state = b_ref[h * pieces + j, at, :] + a_ref[h * pieces + j, at, :] * start_ref[0:1, lanes]
+                    act = jax.nn.gelu(product[:, j * LANES : (j + 1) * LANES], approximate=True)
+                    out_ref[at, lanes] = (state * act).astype(out_ref.dtype)
 
             return 0
 
-        lax.fori_loop(0, blocks, body, 0)
+        lax.fori_loop(0, rows // tall, body, 0)
+
+        @pl.when(t >= split)
+        def _():
+            put_out(t - split).start()
 
     def columns(h):
         return pl.ds(pl.multiple_of(h * channels, channels), channels)
@@ -214,19 +340,19 @@
         return pltpu.make_async_remote_copy(
             src_ref=rec_ref.at[pl.ds(source_rows, lead), columns(h)],
             dst_ref=before_ref.at[:, columns(h)],
-            send_sem=tail_send.at[h], recv_sem=tail_recv.at[h],
+            send_sem=tail_send.at[0], recv_sem=tail_recv.at[h],
             device_id=device, device_id_type=MESH,
         )
 
     def carry_copy(h, device):
         return pltpu.make_async_remote_copy(
             src_ref=carry_ref.at[:, columns(h)], dst_ref=start_ref.at[:, columns(h)],
-            send_sem=carry_send.at[h], recv_sem=carry_recv.at[h],
+            send_sem=carry_send.at[0], recv_sem=carry_recv.at[h],
             device_id=device, device_id_type=MESH,
         )
 
     def send_tail(h):
-        @pl.when(z < nz - 1)
+        @pl.when(z < last)
         def _():
             tail_copy(h, rows - lead, (f, z + 1)).start()
 
@@ -295,13 +421,13 @@
         def _():
             carry_copy(h, (f, z)).wait_recv()
 
-        @pl.when(z < nz - 1)
+        @pl.when(z < last)
         def _():
             end = end_ref[0:1, cols] * start_ref[0:1, cols] + end_ref[1:2, cols]
             carry_ref[:, cols] = jnp.broadcast_to(end, (carry_ref.shape[0], channels))
 
     def send_carry(h):
-        @pl.when(z < nz - 1)
+        @pl.when(z < last)
         def _():
             carry_copy(h, (f, z + 1)).start()
 
@@ -310,72 +436,73 @@
         before_ref[...] = jnp.zeros_like(before_ref)
         start_ref[...] = jnp.zeros_like(start_ref)
 
-    stages = [z_first]
-    for distance in range(1, nz):
-        stages.append(functools.partial(z_hop, distance=distance))
-    stages += [line_done, sides_done, corner_done, gate_done, multiply]
-    lags = list(range(nz)) + [nz - 1, nz, nz + 1, nz + 1, nz + 2]
-    scan_at = gate_steps + nz
+    stages = []
+    for hop in range(nz):
+        stages.append((functools.partial(hop_done, hop=hop), LEAD + GAP * hop))
+    line_lag = LEAD + GAP * reach
+    sides_lag = LEAD + GAP * last
+    stages += [(gate_done, line_lag + 1), (corner_done, sides_lag + GAP), (own_first, 0)]
+    finish = sides_lag + GAP + 1
+    tail_at = finish + 1
+    scan_at = max(tail_at + 1, line_lag + gate_steps)
+    steps = chunks + finish
 
     def on_head(s, first, stage):
-        @pl.when((s >= first) & (s < first + pieces * heads) & ((s - first) % pieces == 0))
-        def _():
-            stage((s - first) // pieces)
+        @pl.when((s >= first) & (s < first + heads))
+        def _():
+            stage(s - first)
 
     def step(s, _):
-        for stage, lag in zip(stages[:-1], lags[:-1]):
+        for stage, lag in stages:
             @pl.when((s >= lag) & (s < chunks + lag))
             def _():
                 stage(s - lag)
 
-        on_head(s, scan_at + 2 + 2 * z, send_carry)
-        on_head(s, nz + 2 + pieces, send_tail)
-
-        @pl.when(s < 4)
-        def _():
-            normalise(tokens_ref, gain_ref, normed_ref, s, 4)
-
-        on_head(s, scan_at + 1 + 2 * z, make_carry)
-
-        @pl.when((s >= lags[-1]) & (s < chunks + lags[-1]))
-        def _():
-            multiply(s - lags[-1])
+        on_head(s, scan_at + 2 + z, send_carry)
+        on_head(s, tail_at, send_tail)
+
+        @pl.when(s == LEAD)
+        def _():
+            token_copy.wait()
+            for copy in small:
+                copy.wait()
+
+        @pl.when((s >= LEAD) & (s < LEAD + NORM_PARTS))
+        def _():
+            normalise(normed_ref, gain_ref, s - LEAD, NORM_PARTS)
+
+        @pl.when((s >= finish) & (s < chunks + finish))
+        def _():
+            multiply(s - finish)
 
         on_head(s, scan_at, scan)
+        on_head(s, scan_at + 1 + z, make_carry)
         return 0
 
-    lax.fori_loop(0, chunks + lags[-1], step, 0)
-
-    def drain(t, _):
-        for k in range(nz):
-            shards_sent = (k + 1 if k < nz - 1 else 0) + (nz - k if k > 0 else 0)
-
-            @pl.when(z == k)
-            def _():
-                sent = w_ref.at[t, pl.ds(0, shards_sent * shard + 3 * line)]
-                pltpu.make_async_copy(sent, sent, send_sem.at[t]).wait()
-
-                @pl.when(t < gate_steps)
-                def _():
-                    sent_gate = table_ref.at[pl.ds(0, shards_sent * piece)]
-                    pltpu.make_async_copy(sent_gate, sent_gate, gate_send.at[t]).wait()
-
-        whole = w_ref.at[t, pl.ds(0, 4 * line)]
-        pltpu.make_async_copy(whole, whole, core_send.at[t]).wait()
-
-        @pl.when(t < gate_steps)
-        def _():
-            others = table_ref.at[pl.ds(0, (nz - 1) * piece)]
-            pltpu.make_async_copy(others, others, gate_core_send.at[t]).wait()
-
-        @pl.when((t < heads) & (z < nz - 1))
-        def _():
-            tail_copy(t, rows - lead, (f, z)).wait_send()
-            carry_copy(t, (f, z)).wait_send()
-
-        return 0
-
-    lax.fori_loop(0, chunks, drain, 0)
+    lax.fori_loop(0, steps, step, 0)
+
+    for k in range(nz):
+        early, late = hop_counts(nz, k, True, False), hop_counts(nz, k, False, False)
+
+        @pl.when(z == k)
+        def _():
+            total = split * (early[2] + late[2])
+            deep = max(n for n in range(1, chunks + 1) if total % n == 0)
+            sent = w_ref.at[pl.ds(0, deep), pl.ds(0, total // deep * shard)]
+            pltpu.make_async_copy(sent, sent, send).wait()
+            sent_gate = table_ref.at[pl.ds(0, early[3] * piece * gate_steps)]
+            pltpu.make_async_copy(sent_gate, sent_gate, gate_send.at[0]).wait()
+
+    whole = w_ref.at[:, pl.ds(0, 4 * line)]
+    pltpu.make_async_copy(whole, whole, core).wait()
+    others = table_ref.at[pl.ds(0, last * piece * gate_steps)]
+    pltpu.make_async_copy(others, others, gate_core_send.at[0]).wait()
+    pltpu.make_async_copy(out_ref, result_ref, out_sem.at[0]).wait()
+
+    @pl.when(z < last)
+    def _():
+        pltpu.make_async_copy(before_ref, before_ref, tail_send.at[0]).wait()
+        pltpu.make_async_copy(carry_ref, carry_ref, carry_send.at[0]).wait()
 
 
 def fused_branch(
@@ -384,10 +511,9 @@
 ):
     rows, width = tokens.shape
     inner = lru_proj.shape[1]
-    chunks = 2 * inner // LANES
     channels = gate_weights.shape[1] // 2
+    chunks = 2 * inner // channels
     heads = inner // channels
-    vmem = pl.BlockSpec(memory_space=pltpu.VMEM)
     any_ = pl.BlockSpec(memory_space=pl.ANY)
     dma = pltpu.SemaphoreType.DMA
     f32, bf16 = jnp.float32, jnp.bfloat16
@@ -395,22 +521,22 @@
     return pl.pallas_call(
         functools.partial(branch_kernel, nz),
         out_shape=jax.ShapeDtypeStruct((rows, inner), bf16),
-        in_specs=[vmem, vmem, any_, any_, any_, vmem, vmem, vmem, vmem],
-        out_specs=vmem,
+        in_specs=[any_] * 9,
+        out_specs=any_,
         scratch_shapes=[
-            pltpu.VMEM((chunks, width, LANES), bf16),
+            pltpu.VMEM((1, width), f32), pltpu.VMEM(conv_weight.shape, f32), pltpu.VMEM((1, inner), f32),
+            pltpu.VMEM(gate_bias.shape, f32), pltpu.VMEM((1, inner), f32), pltpu.VMEM((rows, inner), bf16),
+            pltpu.VMEM((chunks, width, channels), bf16),
             pltpu.VMEM((rows, width), bf16),
             pltpu.VMEM((rows, inner), bf16),
             pltpu.VMEM((gate_weights.shape[0] * nz, 2 * channels), bf16),
             pltpu.VMEM((lead, inner), bf16),
             pltpu.VMEM((lead + rows, channels), f32),
-            pltpu.VMEM((chunks // 2, rows, LANES), f32),
-            pltpu.VMEM((chunks // 2, rows, LANES), f32),
+            pltpu.VMEM((inner // LANES, rows, LANES), f32),
+            pltpu.VMEM((inner // LANES, rows, LANES), f32),
             pltpu.VMEM((8, inner), f32), pltpu.VMEM((8, inner), f32), pltpu.VMEM((8, inner), f32),
-            dma((2,)), dma((chunks,)), dma((chunks,)), dma((chunks // 4,)), dma((chunks // 4,)),
-            dma((heads,)), dma((heads,)),
-            dma((chunks, nz)), dma((chunks // 4, nz)), dma((chunks // 4,)),
-            dma((chunks,)), dma((chunks,)), dma((chunks,)), dma((chunks,)), dma((chunks,)),
+            dma((8,)), dma((1,)), dma((1,)), dma((1,)), dma((1,)), dma((1,)), dma((1,)), dma((1,)),
+            dma((chunks, nz)), dma((chunks,)), dma((chunks,)), dma((chunks // 4,)),
             dma((heads,)), dma((heads,)),
         ],
         compiler_params=pltpu.CompilerParams(
@@ -560,7 +686,7 @@
         P("seq", None), P(), P(),
     )
     nz = mesh.shape["seq"]
-    paired = mesh.shape["fsdp"] == 8 and 1 < nz <= 5
+    paired = mesh.shape["fsdp"] == 8 and 3 < nz <= 5
     return jax.shard_map(
         functools.partial(shards, nz, paired), mesh=mesh, in_specs=placed,
         out_specs=P("fsdp", "seq", None), check_vma=False,

time: 174 us -> 141 us (0.81); the launches traced: 171 us -> 140 us
  Pallas kernels: 167 us -> 137 us
    pallas_call x1, Pallas kernels: 167 us -> 137 us  [fused_branch(): pl.pallas_call(functools.partial(branch_kernel, nz), out_shape=jax.ShapeD...]
where the time goes in v2:
time: 141 us; the launch traced here: 140 us
  Pallas kernels  137 us (97%)
  local copies, waits for them, and re-layouts  3.16 us (2%)
    pallas_call x1, Pallas kernels, fused_branch(): pl.pallas_call(functools.partial(branch_kernel, nz), out_shape=jax.ShapeD...  137 us
    unnamed x1, local copies, waits for them, and re-layouts  3.16 us

profile of v2, /device:TPU:25, one launch (start us, length us, event | category | flops | bytes accessed | tf_op | source)
XLA Modules:
  0.0 140.4 jit_solution(17468073354021948505)
XLA Ops:
  0.0 137.3 %shard_map.91 = bf16[512,2048]{1,0:T(8,128)(2,1)} custom-call(bf16[512,4096]{1,0:T(8,128)(2,1)} %bitcast.6, f32[1,4096]{1,0:T(1,128)} %bitcast.7, bf16[128,2048]{1,0:T(8,128)(2,1)} %lru_ref.1, bf16[128,2048]{1,0:T(8,128)(2,1)} %gelu_ref.1, bf16[512,512]{1,0:T(8,128)(2,1)} %gate_ref.1, f32[4,2048]{1,0:T(4,128)} %weight_in.1, f32[1,2048]{1,0:T(1,128)} %bitcast.8, ...), custom_call_target="tpu_custom_call" | custom-call | tf_op jit(solution)/shard_map/pallas_call | solution.py:521
  137.3 3.2 %copy.11 = bf16[1,512,2048]{2,1,0:T(8,128)(2,1)} copy(bf16[1,512,2048]{2,1,0:T(8,128)(2,1)} %bitcast.5) | data formatting | bytes 4194304

commit v3 on v2

--- a/solution.py
+++ b/solution.py
@@ -9,7 +9,7 @@
 
 MESH = pl.DeviceIdType.MESH
 LANES = 128
-VMEM_BYTES = 66_000_000
+VMEM_BYTES = 58_000_000
 
 
 def normalise(normed_ref, gain_ref, part, parts):
@@ -26,8 +26,7 @@
     lax.fori_loop(part * blocks, (part + 1) * blocks, body, 0)
 
 
-LEAD = 4
-GAP = 2
+LAGS = (4, 7, 10, 12, 13)
 NORM_PARTS = 4
 TALL = 512
 
@@ -68,8 +67,8 @@
     nz,
     tokens_ref, gain_in, lru_ref, gelu_ref, gate_ref,
     weight_in, bias_in, gate_bias_in, decay_in,
-    result_ref,
-    gain_ref, weight_ref, bias_ref, gate_bias_ref, decay_ref, out_ref,
+    out_ref,
+    gain_ref, weight_ref, bias_ref, gate_bias_ref, decay_ref,
     w_ref, normed_ref, rec_ref, table_ref, before_ref, padded_ref, a_ref, b_ref,
     end_ref, carry_ref, start_ref,
     own_sem, out_sem, send_sem, core_send, gate_send, gate_core_send, tail_send, carry_send,
@@ -265,7 +264,7 @@
                 for k in range(nz):
                     @pl.when(z != k)
                     def _():
-                        remote(gate_of(t, k), gate_core_send.at[0], gate_core_recv.at[t], (fc, z)).start()
+                        remote(gate_of(t, k), gate_core_send.at[0], gate_core_recv.at[0], (fc, z)).start()
         if hop == last:
             @pl.when(at_end & (t < split))
             def _():
@@ -280,12 +279,6 @@
             remote(whole_line(t, fx), core, core_recv.at[t], (fc, z)).start()
             remote(whole_line(t, fy), core, core_recv.at[t], (fc, z)).start()
 
-    def gate_done(t):
-        @pl.when(t < gate_steps)
-        def _():
-            others = table_ref.at[pl.ds(0, last * piece)]
-            pltpu.make_async_copy(others, others, gate_core_recv.at[t]).wait()
-
     def corner_done(t):
         @pl.when(at_end & (t < split))
         def _():
@@ -298,9 +291,6 @@
             pltpu.make_async_copy(block, block, far_recv.at[t]).wait()
 
         remote(whole_line(t, fd), core, core_recv.at[t], (fc, z)).start()
-
-    def put_out(h):
-        return pltpu.make_async_copy(out_ref.at[:, columns(h)], result_ref.at[:, columns(h)], out_sem.at[0])
 
     def multiply(t):
         whole = w_ref.at[t, pl.ds(0, 4 * line)]
@@ -328,10 +318,6 @@
             return 0
 
         lax.fori_loop(0, rows // tall, body, 0)
-
-        @pl.when(t >= split)
-        def _():
-            put_out(t - split).start()
 
     def columns(h):
         return pl.ds(pl.multiple_of(h * channels, channels), channels)
@@ -436,15 +422,12 @@
         before_ref[...] = jnp.zeros_like(before_ref)
         start_ref[...] = jnp.zeros_like(start_ref)
 
-    stages = []
-    for hop in range(nz):
-        stages.append((functools.partial(hop_done, hop=hop), LEAD + GAP * hop))
-    line_lag = LEAD + GAP * reach
-    sides_lag = LEAD + GAP * last
-    stages += [(gate_done, line_lag + 1), (corner_done, sides_lag + GAP), (own_first, 0)]
-    finish = sides_lag + GAP + 1
+    hops = [(functools.partial(hop_done, hop=hop), LAGS[hop]) for hop in range(nz)]
+    stages = hops[::-1] + [(corner_done, LAGS[nz]), (own_first, 0)]
+    gates_at = LAGS[reach] + gate_steps
+    finish = LAGS[nz] + 1
     tail_at = finish + 1
-    scan_at = max(tail_at + 1, line_lag + gate_steps)
+    scan_at = max(tail_at + 1, gates_at)
     steps = chunks + finish
 
     def on_head(s, first, stage):
@@ -461,15 +444,20 @@
         on_head(s, scan_at + 2 + z, send_carry)
         on_head(s, tail_at, send_tail)
 
-        @pl.when(s == LEAD)
+        @pl.when(s == gates_at)
+        def _():
+            others = table_ref.at[pl.ds(0, last * piece * gate_steps)]
+            pltpu.make_async_copy(others, others, gate_core_recv.at[0]).wait()
+
+        @pl.when(s == LAGS[0])
         def _():
             token_copy.wait()
             for copy in small:
                 copy.wait()
 
-        @pl.when((s >= LEAD) & (s < LEAD + NORM_PARTS))
-        def _():
-            normalise(normed_ref, gain_ref, s - LEAD, NORM_PARTS)
+        @pl.when((s >= LAGS[0]) & (s < LAGS[0] + NORM_PARTS))
+        def _():
+            normalise(normed_ref, gain_ref, s - LAGS[0], NORM_PARTS)
 
         @pl.when((s >= finish) & (s < chunks + finish))
         def _():
@@ -497,7 +485,6 @@
     pltpu.make_async_copy(whole, whole, core).wait()
     others = table_ref.at[pl.ds(0, last * piece * gate_steps)]
     pltpu.make_async_copy(others, others, gate_core_send.at[0]).wait()
-    pltpu.make_async_copy(out_ref, result_ref, out_sem.at[0]).wait()
 
     @pl.when(z < last)
     def _():
@@ -520,12 +507,12 @@
     lead = 16
     return pl.pallas_call(
         functools.partial(branch_kernel, nz),
-        out_shape=jax.ShapeDtypeStruct((rows, inner), bf16),
+        out_shape=pltpu.VMEM((rows, inner), bf16),
         in_specs=[any_] * 9,
-        out_specs=any_,
+        out_specs=pl.BlockSpec(memory_space=pltpu.VMEM),
         scratch_shapes=[
             pltpu.VMEM((1, width), f32), pltpu.VMEM(conv_weight.shape, f32), pltpu.VMEM((1, inner), f32),
-            pltpu.VMEM(gate_bias.shape, f32), pltpu.VMEM((1, inner), f32), pltpu.VMEM((rows, inner), bf16),
+            pltpu.VMEM(gate_bias.shape, f32), pltpu.VMEM((1, inner), f32),
             pltpu.VMEM((chunks, width, channels), bf16),
             pltpu.VMEM((rows, width), bf16),
             pltpu.VMEM((rows, inner), bf16),
@@ -536,7 +523,7 @@
             pltpu.VMEM((inner // LANES, rows, LANES), f32),
             pltpu.VMEM((8, inner), f32), pltpu.VMEM((8, inner), f32), pltpu.VMEM((8, inner), f32),
             dma((8,)), dma((1,)), dma((1,)), dma((1,)), dma((1,)), dma((1,)), dma((1,)), dma((1,)),
-            dma((chunks, nz)), dma((chunks,)), dma((chunks,)), dma((chunks // 4,)),
+            dma((chunks, nz)), dma((chunks,)), dma((chunks,)), dma((1,)),
             dma((heads,)), dma((heads,)),
         ],
         compiler_params=pltpu.CompilerParams(
@@ -686,7 +673,7 @@
         P("seq", None), P(), P(),
     )
     nz = mesh.shape["seq"]
-    paired = mesh.shape["fsdp"] == 8 and 3 < nz <= 5
+    paired = mesh.shape["fsdp"] == 8 and nz == len(LAGS) - 1
     return jax.shard_map(
         functools.partial(shards, nz, paired), mesh=mesh, in_specs=placed,
         out_specs=P("fsdp", "seq", None), check_vma=False,

time: 141 us -> 139 us (0.986)
  local copies, waits for them, and re-layouts: 3.16 us -> 1.32 us
    unnamed x1, local copies, waits for them, and re-layouts: 3.16 us -> 1.32 us
where the time goes in v3:
time: 139 us
  Pallas kernels  138 us (99%)
    pallas_call x1, Pallas kernels, fused_branch(): pl.pallas_call(functools.partial(branch_kernel, nz), out_shape=pltpu.VMEM...  138 us

profile of v3, /device:TPU:25, one launch (start us, length us, event | category | flops | bytes accessed | tf_op | source)
XLA Modules:
  0.0 138.8 jit_solution(4334313772382220266)
XLA Ops:
  0.0 137.5 %shard_map.91 = bf16[512,2048]{1,0:T(8,128)(2,1)S(1)} custom-call(bf16[512,4096]{1,0:T(8,128)(2,1)} %bitcast.6, f32[1,4096]{1,0:T(1,128)} %bitcast.7, bf16[128,2048]{1,0:T(8,128)(2,1)} %lru_ref.1, bf16[128,2048]{1,0:T(8,128)(2,1)} %gelu_ref.1, bf16[512,512]{1,0:T(8,128)(2,1)} %gate_ref.1, f32[4,2048]{1,0:T(4,128)} %weight_in.1, f32[1,2048]{1,0:T(1,128)} %bitcast.8, ...), custom_call_target="tpu_custom_call" | custom-call | tf_op jit(solution)/shard_map/pallas_call | solution.py:508
  137.5 1.3 copy.11

commit v4 on v3

--- a/solution.py
+++ b/solution.py
@@ -26,9 +26,11 @@
     lax.fori_loop(part * blocks, (part + 1) * blocks, body, 0)
 
 
-LAGS = (4, 7, 10, 12, 13)
+LAGS = (5, 9, 12, 14, 15)
 NORM_PARTS = 4
 TALL = 512
+EXTRA = 1
+SLACK = 0
 
 
 def hop_counts(nz, k, early, gates):
@@ -84,6 +86,7 @@
     half = shard // 2
     chunks, _, wide = w_ref.shape
     split = chunks // 2
+    early_chunks = split + EXTRA
     gate_rows = gate_ref.shape[0]
     gate_steps = split // 2
     piece = gate_rows // 2 // gate_steps
@@ -154,21 +157,24 @@
         first = source * gate_rows + c * (gate_rows // 2) + t * piece
         return table_ref.at[pl.ds(pl.multiple_of(first, piece), piece)]
 
-    send, core = send_sem.at[0], core_send.at[0]
+    core = core_send.at[0]
+
+    def sender(t):
+        return send_sem.at[jnp.where(t < early_chunks, 0, 1)]
 
     def along_z(t, k, target, distance):
-        remote(unit(t, f, k), send, hop_recv.at[t, distance - 1], (f, target)).start()
+        remote(unit(t, f, k), sender(t), hop_recv.at[t, distance - 1], (f, target)).start()
 
         @pl.when(t < gate_steps)
         def _():
             remote(gate_of(t, k), gate_send.at[0], hop_recv.at[t, distance - 1], (f, target)).start()
 
     def across(t, k, hop):
-        remote(unit(t, f, k), send, hop_recv.at[t, hop], (fx, z)).start()
-        remote(unit(t, f, k), send, hop_recv.at[t, hop], (fy, z)).start()
+        remote(unit(t, f, k), sender(t), hop_recv.at[t, hop], (fx, z)).start()
+        remote(unit(t, f, k), sender(t), hop_recv.at[t, hop], (fy, z)).start()
 
     def diagonal(t, k, target, distance):
-        remote(unit(t, fd, k), send, hop_recv.at[t, distance + 1], (f, target)).start()
+        remote(unit(t, fd, k), sender(t), hop_recv.at[t, distance + 1], (f, target)).start()
 
     def wait_hop(t, hop):
         sizes = {}
@@ -181,7 +187,7 @@
                 continue
             chosen = False
             for (early, gates), ks in places.items():
-                when = (t < gate_steps) if gates else ((t >= gate_steps) & (t < split)) if early else (t >= split)
+                when = (t < gate_steps) if gates else ((t >= gate_steps) & (t < early_chunks)) if early else (t >= early_chunks)
                 if len(ks) < nz:
                     there = z == ks[0]
                     for k in ks[1:]:
@@ -224,7 +230,7 @@
             across(t, z + distance, last)
 
     def d_hop(t, distance):
-        onward = (t >= split) | (distance + 1 < reach)
+        onward = (t >= early_chunks) | (distance + 1 < reach)
 
         @pl.when((z >= distance) & (z < last) & (onward | (z + 1 < last)))
         def _():
@@ -242,8 +248,8 @@
         if hop + 1 < last:
             z_hop(t, hop + 1)
         if hop == 0:
-            remote(unit(t, fx, z, 0, half), send, hop_recv.at[t, 1], (fy, z)).start()
-            remote(unit(t, fy, z, half, half), send, hop_recv.at[t, 1], (fx, z)).start()
+            remote(unit(t, fx, z, 0, half), sender(t), hop_recv.at[t, 1], (fy, z)).start()
+            remote(unit(t, fy, z, half, half), sender(t), hop_recv.at[t, 1], (fx, z)).start()
         if hop == 1:
             @pl.when(z > 0)
             def _():
@@ -266,26 +272,26 @@
                     def _():
                         remote(gate_of(t, k), gate_core_send.at[0], gate_core_recv.at[0], (fc, z)).start()
         if hop == last:
-            @pl.when(at_end & (t < split))
-            def _():
-                remote(unit(t, fx, far), send, far_recv.at[t], (fy, z)).start()
-                remote(unit(t, fy, middle), send, far_recv.at[t], (fx, z)).start()
-
-            @pl.when(at_end & (t >= split))
-            def _():
-                remote(unit(t, fx, far, 0, half), send, far_recv.at[t], (fy, z)).start()
-                remote(unit(t, fy, far, half, half), send, far_recv.at[t], (fx, z)).start()
+            @pl.when(at_end & (t < early_chunks))
+            def _():
+                remote(unit(t, fx, far), sender(t), far_recv.at[t], (fy, z)).start()
+                remote(unit(t, fy, middle), sender(t), far_recv.at[t], (fx, z)).start()
+
+            @pl.when(at_end & (t >= early_chunks))
+            def _():
+                remote(unit(t, fx, far, 0, half), sender(t), far_recv.at[t], (fy, z)).start()
+                remote(unit(t, fy, far, half, half), sender(t), far_recv.at[t], (fx, z)).start()
 
             remote(whole_line(t, fx), core, core_recv.at[t], (fc, z)).start()
             remote(whole_line(t, fy), core, core_recv.at[t], (fc, z)).start()
 
     def corner_done(t):
-        @pl.when(at_end & (t < split))
+        @pl.when(at_end & (t < early_chunks))
         def _():
             block = w_ref.at[0, pl.ds(0, 2 * shard)]
             pltpu.make_async_copy(block, block, far_recv.at[t]).wait()
 
-        @pl.when(at_end & (t >= split))
+        @pl.when(at_end & (t >= early_chunks))
         def _():
             block = w_ref.at[0, pl.ds(0, shard)]
             pltpu.make_async_copy(block, block, far_recv.at[t]).wait()
@@ -311,7 +317,7 @@
                 h = jnp.maximum(t - split, 0)
                 for j in range(pieces):
                     lanes = pl.ds(pl.multiple_of(h * channels + j * LANES, LANES), LANES)
-                    state = b_ref[h * pieces + j, at, :] + a_ref[h * pieces + j, at, :] * start_ref[0:1, lanes]
+                    state = b_ref[h * pieces + j, at, :] + a_ref[h * pieces + j, at, :] * start_ref[h, :, j * LANES : (j + 1) * LANES]
                     act = jax.nn.gelu(product[:, j * LANES : (j + 1) * LANES], approximate=True)
                     out_ref[at, lanes] = (state * act).astype(out_ref.dtype)
 
@@ -332,7 +338,7 @@
 
     def carry_copy(h, device):
         return pltpu.make_async_remote_copy(
-            src_ref=carry_ref.at[:, columns(h)], dst_ref=start_ref.at[:, columns(h)],
+            src_ref=carry_ref.at[h], dst_ref=start_ref.at[h],
             send_sem=carry_send.at[0], recv_sem=carry_recv.at[h],
             device_id=device, device_id_type=MESH,
         )
@@ -409,8 +415,7 @@
 
         @pl.when(z < last)
         def _():
-            end = end_ref[0:1, cols] * start_ref[0:1, cols] + end_ref[1:2, cols]
-            carry_ref[:, cols] = jnp.broadcast_to(end, (carry_ref.shape[0], channels))
+            carry_ref[h] = end_ref[0:1, cols] * start_ref[h] + end_ref[1:2, cols]
 
     def send_carry(h):
         @pl.when(z < last)
@@ -427,7 +432,7 @@
     gates_at = LAGS[reach] + gate_steps
     finish = LAGS[nz] + 1
     tail_at = finish + 1
-    scan_at = max(tail_at + 1, gates_at)
+    scan_at = max(tail_at + 1 + SLACK, gates_at)
     steps = chunks + finish
 
     def on_head(s, first, stage):
@@ -436,13 +441,13 @@
             stage(s - first)
 
     def step(s, _):
+        on_head(s, scan_at + 2 + z, send_carry)
+        on_head(s, tail_at, send_tail)
+
         for stage, lag in stages:
             @pl.when((s >= lag) & (s < chunks + lag))
             def _():
                 stage(s - lag)
-
-        on_head(s, scan_at + 2 + z, send_carry)
-        on_head(s, tail_at, send_tail)
 
         @pl.when(s == gates_at)
         def _():
@@ -474,10 +479,9 @@
 
         @pl.when(z == k)
         def _():
-            total = split * (early[2] + late[2])
-            deep = max(n for n in range(1, chunks + 1) if total % n == 0)
-            sent = w_ref.at[pl.ds(0, deep), pl.ds(0, total // deep * shard)]
-            pltpu.make_async_copy(sent, sent, send).wait()
+            for i, (depth, counts) in enumerate(((early_chunks, early), (chunks - early_chunks, late))):
+                sent = w_ref.at[pl.ds(0, depth), pl.ds(0, counts[2] * shard)]
+                pltpu.make_async_copy(sent, sent, send_sem.at[i]).wait()
             sent_gate = table_ref.at[pl.ds(0, early[3] * piece * gate_steps)]
             pltpu.make_async_copy(sent_gate, sent_gate, gate_send.at[0]).wait()
 
@@ -504,7 +508,7 @@
     any_ = pl.BlockSpec(memory_space=pl.ANY)
     dma = pltpu.SemaphoreType.DMA
     f32, bf16 = jnp.float32, jnp.bfloat16
-    lead = 16
+    lead = 8
     return pl.pallas_call(
         functools.partial(branch_kernel, nz),
         out_shape=pltpu.VMEM((rows, inner), bf16),
@@ -521,8 +525,8 @@
             pltpu.VMEM((lead + rows, channels), f32),
             pltpu.VMEM((inner // LANES, rows, LANES), f32),
             pltpu.VMEM((inner // LANES, rows, LANES), f32),
-            pltpu.VMEM((8, inner), f32), pltpu.VMEM((8, inner), f32), pltpu.VMEM((8, inner), f32),
-            dma((8,)), dma((1,)), dma((1,)), dma((1,)), dma((1,)), dma((1,)), dma((1,)), dma((1,)),
+            pltpu.VMEM((8, inner), f32), pltpu.VMEM((heads, 1, channels), f32), pltpu.VMEM((heads, 1, channels), f32),
+            dma((8,)), dma((1,)), dma((2,)), dma((1,)), dma((1,)), dma((1,)), dma((1,)), dma((1,)),
             dma((chunks, nz)), dma((chunks,)), dma((chunks,)), dma((1,)),
             dma((heads,)), dma((heads,)),
         ],

time: 139 us -> 134 us (0.964)
  Pallas kernels: 138 us -> 132 us
    pallas_call x1, Pallas kernels: 138 us -> 132 us  [fused_branch(): pl.pallas_call(functools.partial(branch_kernel, nz), out_shape=pltpu.VMEM...]
where the time goes in v4:
time: 134 us; the launch traced here: 133 us
  Pallas kernels  132 us (99%)
    pallas_call x1, Pallas kernels, fused_branch(): pl.pallas_call(functools.partial(branch_kernel, nz), out_shape=pltpu.VMEM...  132 us

profile of v4, /device:TPU:25, one launch (start us, length us, event | category | flops | bytes accessed | tf_op | source)
XLA Modules:
  0.0 132.9 jit_solution(2381461944237151335)
XLA Ops:
  0.0 131.6 %shard_map.91 = bf16[512,2048]{1,0:T(8,128)(2,1)S(1)} custom-call(bf16[512,4096]{1,0:T(8,128)(2,1)} %bitcast.6, f32[1,4096]{1,0:T(1,128)} %bitcast.7, bf16[128,2048]{1,0:T(8,128)(2,1)} %lru_ref.1, bf16[128,2048]{1,0:T(8,128)(2,1)} %gelu_ref.1, bf16[512,512]{1,0:T(8,128)(2,1)} %gate_ref.1, f32[4,2048]{1,0:T(4,128)} %weight_in.1, f32[1,2048]{1,0:T(1,128)} %bitcast.8, ...), custom_call_target="tpu_custom_call" | custom-call | tf_op jit(solution)/shard_map/pallas_call | solution.py:512
  131.6 1.3 copy.11

commit v5 on v4

--- a/solution.py
+++ b/solution.py
@@ -26,7 +26,7 @@
     lax.fori_loop(part * blocks, (part + 1) * blocks, body, 0)
 
 
-LAGS = (5, 9, 12, 14, 15)
+LAGS = (6, 11, 14, 16, 17)
 NORM_PARTS = 4
 TALL = 512
 EXTRA = 1

time: 134 us -> 134 us (level)
  no operation moved by 1% of the time
where the time goes in v5:
time: 134 us; the launch traced here: 133 us
  Pallas kernels  131 us (98%)
    pallas_call x1, Pallas kernels, fused_branch(): pl.pallas_call(functools.partial(branch_kernel, nz), out_shape=pltpu.VMEM...  131 us

profile of v5, /device:TPU:25, one launch (start us, length us, event | category | flops | bytes accessed | tf_op | source)
XLA Modules:
  0.0 132.8 jit_solution(13692304934582152492)
XLA Ops:
  0.0 131.5 %shard_map.91 = bf16[512,2048]{1,0:T(8,128)(2,1)S(1)} custom-call(bf16[512,4096]{1,0:T(8,128)(2,1)} %bitcast.6, f32[1,4096]{1,0:T(1,128)} %bitcast.7, bf16[128,2048]{1,0:T(8,128)(2,1)} %lru_ref.1, bf16[128,2048]{1,0:T(8,128)(2,1)} %gelu_ref.1, bf16[512,512]{1,0:T(8,128)(2,1)} %gate_ref.1, f32[4,2048]{1,0:T(4,128)} %weight_in.1, f32[1,2048]{1,0:T(1,128)} %bitcast.8, ...), custom_call_target="tpu_custom_call" | custom-call | tf_op jit(solution)/shard_map/pallas_call | solution.py:512
  131.5 1.3 copy.11

commit v6 on v5

--- a/solution.py
+++ b/solution.py
@@ -29,7 +29,8 @@
 LAGS = (6, 11, 14, 16, 17)
 NORM_PARTS = 4
 TALL = 512
-EXTRA = 1
+EXTRA = 2
+LONG = 2
 SLACK = 0
 
 
@@ -87,6 +88,7 @@
     chunks, _, wide = w_ref.shape
     split = chunks // 2
     early_chunks = split + EXTRA
+    long_from = chunks - LONG
     gate_rows = gate_ref.shape[0]
     gate_steps = split // 2
     piece = gate_rows // 2 // gate_steps
@@ -160,7 +162,7 @@
     core = core_send.at[0]
 
     def sender(t):
-        return send_sem.at[jnp.where(t < early_chunks, 0, 1)]
+        return send_sem.at[jnp.where(t < early_chunks, 0, jnp.where(t < long_from, 1, 2))]
 
     def along_z(t, k, target, distance):
         remote(unit(t, f, k), sender(t), hop_recv.at[t, distance - 1], (f, target)).start()
@@ -174,20 +176,39 @@
         remote(unit(t, f, k), sender(t), hop_recv.at[t, hop], (fy, z)).start()
 
     def diagonal(t, k, target, distance):
-        remote(unit(t, fd, k), sender(t), hop_recv.at[t, distance + 1], (f, target)).start()
+        if distance < reach:
+            remote(unit(t, fd, k), sender(t), hop_recv.at[t, distance + 1], (f, target)).start()
+            return
+        apart = (t >= long_from) & (target > 0) & (target < last)
+
+        @pl.when(apart)
+        def _():
+            remote(unit(t, fd, k), sender(t), far_recv.at[t], (f, target)).start()
+
+        @pl.when(jnp.logical_not(apart))
+        def _():
+            remote(unit(t, fd, k), sender(t), hop_recv.at[t, distance + 1], (f, target)).start()
 
     def wait_hop(t, hop):
+        spans = (
+            (True, True, 0, t < gate_steps),
+            (True, False, 0, (t >= gate_steps) & (t < early_chunks)),
+            (False, False, 0, (t >= early_chunks) & (t < long_from)),
+            (False, False, 1, t >= long_from),
+        )
         sizes = {}
         for k in range(nz):
-            for early, gates in ((True, True), (True, False), (False, False)):
+            for i, (early, gates, apart, _) in enumerate(spans):
                 count = hop_counts(nz, k, early, gates)[0].get(hop, 0)
-                sizes.setdefault(count, {}).setdefault((early, gates), []).append(k)
+                if apart and hop == last and 0 < k < last:
+                    count -= 1
+                sizes.setdefault(count, {}).setdefault(i, []).append(k)
         for count, places in sizes.items():
             if count == 0:
                 continue
             chosen = False
-            for (early, gates), ks in places.items():
-                when = (t < gate_steps) if gates else ((t >= gate_steps) & (t < early_chunks)) if early else (t >= early_chunks)
+            for i, ks in places.items():
+                when = spans[i][3]
                 if len(ks) < nz:
                     there = z == ks[0]
                     for k in ks[1:]:
@@ -242,6 +263,14 @@
 
     far = last - z
     middle = jnp.where(z == 0, reach, 1)
+
+    def pass_far(t):
+        for k, source, target in ((1, last, 0), (reach, 0, last)):
+            @pl.when((t >= long_from) & (z == k))
+            def _():
+                block = unit(t, fd, source)
+                pltpu.make_async_copy(block, block, far_recv.at[t]).wait()
+                remote(block, sender(t), far_recv.at[t], (f, target)).start()
 
     def hop_done(t, hop):
         wait_hop(t, hop)
@@ -277,7 +306,7 @@
                 remote(unit(t, fx, far), sender(t), far_recv.at[t], (fy, z)).start()
                 remote(unit(t, fy, middle), sender(t), far_recv.at[t], (fx, z)).start()
 
-            @pl.when(at_end & (t >= early_chunks))
+            @pl.when(at_end & (t >= early_chunks) & (t < long_from))
             def _():
                 remote(unit(t, fx, far, 0, half), sender(t), far_recv.at[t], (fy, z)).start()
                 remote(unit(t, fy, far, half, half), sender(t), far_recv.at[t], (fx, z)).start()
@@ -428,7 +457,7 @@
         start_ref[...] = jnp.zeros_like(start_ref)
 
     hops = [(functools.partial(hop_done, hop=hop), LAGS[hop]) for hop in range(nz)]
-    stages = hops[::-1] + [(corner_done, LAGS[nz]), (own_first, 0)]
+    stages = [(pass_far, LAGS[reach] + 1)] + hops[::-1] + [(corner_done, LAGS[nz]), (own_first, 0)]
     gates_at = LAGS[reach] + gate_steps
     finish = LAGS[nz] + 1
     tail_at = finish + 1
@@ -479,8 +508,10 @@
 
         @pl.when(z == k)
         def _():
-            for i, (depth, counts) in enumerate(((early_chunks, early), (chunks - early_chunks, late))):
-                sent = w_ref.at[pl.ds(0, depth), pl.ds(0, counts[2] * shard)]
+            through = late[2] - 1 if k in (0, last) else late[2] + int(k == 1) + int(k == reach)
+            groups = ((early_chunks, early[2]), (long_from - early_chunks, late[2]), (LONG, through))
+            for i, (depth, count) in enumerate(groups):
+                sent = w_ref.at[pl.ds(0, depth), pl.ds(0, count * shard)]
                 pltpu.make_async_copy(sent, sent, send_sem.at[i]).wait()
             sent_gate = table_ref.at[pl.ds(0, early[3] * piece * gate_steps)]
             pltpu.make_async_copy(sent_gate, sent_gate, gate_send.at[0]).wait()
@@ -526,7 +557,7 @@
             pltpu.VMEM((inner // LANES, rows, LANES), f32),
             pltpu.VMEM((inner // LANES, rows, LANES), f32),
             pltpu.VMEM((8, inner), f32), pltpu.VMEM((heads, 1, channels), f32), pltpu.VMEM((heads, 1, channels), f32),
-            dma((8,)), dma((1,)), dma((2,)), dma((1,)), dma((1,)), dma((1,)), dma((1,)), dma((1,)),
+            dma((8,)), dma((1,)), dma((3,)), dma((1,)), dma((1,)), dma((1,)), dma((1,)), dma((1,)),
             dma((chunks, nz)), dma((chunks,)), dma((chunks,)), dma((1,)),
             dma((heads,)), dma((heads,)),
         ],

time: 134 us -> 134 us (level)
  no operation moved by 1% of the time
where the time goes in v6:
time: 134 us; the launch traced here: 133 us
  Pallas kernels  131 us (98%)
    pallas_call x1, Pallas kernels, fused_branch(): pl.pallas_call(functools.partial(branch_kernel, nz), out_shape=pltpu.VMEM...  131 us

profile of v6, /device:TPU:25, one launch (start us, length us, event | category | flops | bytes accessed | tf_op | source)
XLA Modules:
  0.0 132.7 jit_solution(4799361824424124622)
XLA Ops:
  0.0 131.3 %shard_map.91 = bf16[512,2048]{1,0:T(8,128)(2,1)S(1)} custom-call(bf16[512,4096]{1,0:T(8,128)(2,1)} %bitcast.6, f32[1,4096]{1,0:T(1,128)} %bitcast.7, bf16[128,2048]{1,0:T(8,128)(2,1)} %lru_ref.1, bf16[128,2048]{1,0:T(8,128)(2,1)} %gelu_ref.1, bf16[512,512]{1,0:T(8,128)(2,1)} %gate_ref.1, f32[4,2048]{1,0:T(4,128)} %weight_in.1, f32[1,2048]{1,0:T(1,128)} %bitcast.8, ...), custom_call_target="tpu_custom_call" | custom-call | tf_op jit(solution)/shard_map/pallas_call | solution.py:543
  131.3 1.3 copy.11
